TPU v7x, 16 devices: a whole 2x2x2 slice. The times are simulated.
16 devices in a mesh: tp: 2 (over z), dp: 8 (over y, x, core).
Axes of the slice: x: 2, y: 2, z: 2, core: 2. Of those that a mesh axis runs over, the one named last changes fastest.
Arguments:
- hidden_in: bfloat16 [4096, 4096], P('dp')
- labels: int32 [4096], P('dp')
- loss_mask: int32 [4096], P('dp')
- norm_gamma: bfloat16 [4096], replicated
- w_out: bfloat16 [4096, 32000], P(None, 'tp')
Outputs:
- output 1: float32 [], replicated
- output 2: bfloat16 [4096, 4096], P('dp')
- output 3: float32 [4096, 32000], P('dp', 'tp')
- output 4: float32 [4096], replicated
All inputs are finite; a program needn't handle non-finite values.
Results may differ from a plain program's by a relative error of at most 0.001.
Values sent between devices are 32-bit elements.
A program may use at most 1 GiB of HBM per device.

v0:
```python
import jax
import jax.numpy as jnp
from jax import lax
from jax.sharding import PartitionSpec as P

NORM_EPS = 1e-5


def solution(mesh):
    def local_step(hidden_in, labels, loss_mask, norm_gamma, w_local):
        vocab_local = w_local.shape[1]
        hid_f32 = hidden_in.astype(jnp.float32)
        gain_f32 = norm_gamma.astype(jnp.float32)
        inv_rms = lax.rsqrt(jnp.mean(hid_f32 * hid_f32, axis=-1, keepdims=True) + NORM_EPS)
        x_hat = hid_f32 * inv_rms
        normed = (x_hat * gain_f32).astype(jnp.bfloat16)
        logits = jnp.dot(normed, w_local, preferred_element_type=jnp.float32)
        row_max = lax.pmax(jnp.max(logits, axis=-1, keepdims=True), "tp")
        col_ids = lax.axis_index("tp") * vocab_local + jnp.arange(vocab_local, dtype=jnp.int32)
        one_hot = labels[:, None] == col_ids[None, :]
        shifted = jnp.exp(logits - row_max)
        sum_exp, target = lax.psum((jnp.sum(shifted, axis=-1, keepdims=True), jnp.sum(jnp.where(one_hot, logits, 0.0), axis=-1, keepdims=True)), "tp")
        log_z = row_max + jnp.log(sum_exp)
        mask_f32 = loss_mask.astype(jnp.float32)[:, None]
        count, loss_sum = lax.psum((jnp.sum(mask_f32), jnp.sum(mask_f32 * (log_z - target))), "dp")
        loss = loss_sum / count
        tok_scale = mask_f32 / count
        d_logits = ((shifted * (1.0 / sum_exp) - one_hot.astype(jnp.float32)) * tok_scale).astype(jnp.bfloat16)
        w_grad_part = lax.dot_general(normed, d_logits, (((0,), (0,)), ((), ())), preferred_element_type=jnp.float32)
        d_w_out = lax.psum_scatter(w_grad_part, "dp", scatter_dimension=0, tiled=True)
        dn_part = lax.dot_general(d_logits, w_local, (((1,), (1,)), ((), ())), preferred_element_type=jnp.float32)
        d_normed = lax.psum(dn_part, "tp")
        d_gamma = lax.psum(jnp.sum(d_normed * x_hat, axis=0), "dp")
        d_hat = d_normed * gain_f32
        d_hidden = (inv_rms * (d_hat - x_hat * jnp.mean(d_hat * x_hat, axis=-1, keepdims=True))).astype(jnp.bfloat16)
        return (loss, d_hidden, d_w_out, d_gamma)

    return jax.shard_map(local_step, mesh=mesh, in_specs=(P("dp", None), P("dp"), P("dp"), P(), P(None, "tp")), out_specs=(P(), P("dp", None), P("dp", "tp"), P()), check_vma=False)
```

profile of v0, /device:TPU:0, one launch (start us, length us, event | category | flops | bytes accessed | tf_op | source)
XLA Modules:
  0.0 1773.6 jit_solution(10372243733902330288)
XLA Ops:
  8.0 0.0 all-reduce.4.cloned.1.call-start
  8.0 1.3 convert_reduce_fusion
  9.3 0.7 convert_element_type.21
  10.0 16.1 psum.45
  26.1 1.3 broadcast_divide_fusion
  27.4 3.1 fusion.15
  30.5 0.0 copy-start
  30.5 0.7 convert_element_type.23
  31.2 0.0 copy-start.2
  31.2 0.0 copy-start.4
  31.2 79.4 %fusion.23 = (f32[512]{0:T(512)S(1)}, f32[512,16000]{1,0:T(8,128)}) fusion(bf16[4096,16000]{1,0:T(8,128)(2,1)} %param.9, bf16[512,4096]{1,0:T(8,128)(2,1)} %param.5, f32[4096]{0:T(1024)S(1)} %convert_element_type.23, f32[512]{0:T(512)S(1)} %add_rsqrt_fusion), kind=kOutput, calls=%fused_computation.31 | convolution fusion | flops 67125444608 | bytes 168054784 | tf_op jit(solution)/shard_map/dot_general | solution.py:17
  110.6 0.0 copy-done
  110.6 0.0 copy-done.2
  110.6 4.9 pmax.7
  115.5 0.0 copy-done.4
  115.5 16.7 fusion.4
  132.3 5.1 all-reduce.1
  137.4 0.6 broadcast_divide_fusion.1
  138.0 20.5 %fusion.36 = bf16[512,16000]{1,0:T(8,128)(2,1)} fusion(f32[512,16000]{1,0:T(8,128)} %get-tuple-element.15, f32[512]{0:T(512)S(1)} %broadcast_divide_fusion, f32[512]{0:T(512)S(1)} %bitcast.14, s32[16000]{0:T(1024)S(1)} %iota_add_fusion, f32[512]{0:T(512)S(1)} %bitcast.12, s32[512]{0:T(512)S(1)} %copy-done.4), kind=kLoop, calls=%fused_computation.5.clone.1.clone.1 | loop fusion | flops 57344000 | bytes 49224192 | tf_op jit(solution)/shard_map/dot_general | solution.py:31
  158.5 0.0 copy-start.1
  158.5 0.0 copy-start.3
  158.5 80.4 %fusion.21 = f32[512,4096]{1,0:T(8,128)} fusion(bf16[4096,16000]{1,0:T(8,128)(2,1)} %param.9, bf16[512,16000]{1,0:T(8,128)(2,1)} %fusion.36), kind=kOutput, calls=%fused_computation.30 | convolution fusion | flops 67108864000 | bytes 155844608 | tf_op jit(solution)/shard_map/dot_general | solution.py:31
  239.0 0.0 all-reduce.4.cloned.1.call-update
  239.0 0.0 reduce-scatter.2.cloned.1.call-start
  239.0 0.0 copy-done.1
  239.0 0.0 copy-done.3
  239.1 105.3 %fusion.16 = f32[4096,16000]{1,0:T(8,128)} fusion(bf16[512,4096]{1,0:T(8,128)(2,1)} %param.5, f32[4096]{0:T(1024)S(1)} %copy-done.3, f32[512]{0:T(512)S(1)} %copy-done.1, f32[512,16000]{1,0:T(8,128)} %get-tuple-element.15, f32[512]{0:T(512)S(1)} %broadcast_divide_fusion, f32[512]{0:T(512)S(1)} %bitcast.15, s32[16000]{0:T(1024)S(1)} %iota_add_fusion, ...), kind=kOutput, calls=%fused_computation.21 | convolution fusion | flops 67174596608 | bytes 299196928 | tf_op jit(solution)/shard_map/dot_general | solution.py:29
  344.4 0.0 reduce-scatter.2.cloned.1.call-update
  344.4 88.0 %all-reduce.4.cloned.1.call-done = f32[512,4096]{1,0:T(8,128)} async-done(((f32[512,4096]{1,0:T(8,128)}), f32[512,4096]{1,0:T(8,128)}) %all-reduce.4.cloned.1.call-update) | async-done | bytes 8388624 | tf_op jit(solution)/shard_map/psum | solution.py:32
  432.4 5.9 fusion.14
  438.3 25.0 %all-reduce = (f32[]{:T(128)}, f32[4096]{0:T(1024)}) all-reduce(f32[]{:T(128)} %get-tuple-element.13, f32[4096]{0:T(1024)S(1)} %get-tuple-element.6), channel_id=1, replica_groups=mesh['tp'=2,'dp'=8] {'dp'}, use_global_device_ids=true, to_apply=%region_8.9 | all-reduce | flops 4097 | bytes 32776 | tf_op jit(solution)/shard_map/psum | solution.py:25
  464.6 7.2 fusion.13
  471.8 1293.3 %reduce-scatter.2.cloned.1.call-done = f32[512,16000]{1,0:T(8,128)} async-done(((f32[4096,16000]{1,0:T(8,128)}), f32[512,16000]{1,0:T(8,128)}) %reduce-scatter.2.cloned.1.call-update) | async-done | bytes 32768016 | tf_op jit(solution)/shard_map/reduce_scatter | solution.py:30
  (3 shorter events, 0.0 us)
Async XLA Ops:
  8.0 424.4 %all-reduce.4.cloned.1.call-start = ((), (), s32[]{:S(2)}) async-start(), calls=%async_computation.1 | async-start | bytes 16777216 | tf_op jit(solution)/shard_map/psum | solution.py:32
  30.5 80.1 %copy-start = (f32[512]{0:T(512)}, f32[512]{0:T(512)S(1)}, u32[]{:S(2)}) copy-start(f32[512]{0:T(512)S(1)} %add_rsqrt_fusion) | copy-start | bytes 6148
  31.2 79.4 %copy-start.2 = (f32[4096]{0:T(1024)}, f32[4096]{0:T(1024)S(1)}, u32[]{:S(2)}) copy-start(f32[4096]{0:T(1024)S(1)} %convert_element_type.23) | copy-start | bytes 49156
  31.2 84.3 %copy-start.4 = (s32[512]{0:T(512)S(1)}, s32[512]{0:T(512)}, u32[]{:S(2)}) copy-start(s32[512]{0:T(512)} %param.6) | copy-start | bytes 6148
  158.5 80.5 %copy-start.1 = (f32[512]{0:T(512)S(1)}, f32[512]{0:T(512)}, u32[]{:S(2)}) copy-start(f32[512]{0:T(512)} %copy-done) | copy-start | bytes 6148
  158.5 80.5 %copy-start.3 = (f32[4096]{0:T(1024)S(1)}, f32[4096]{0:T(1024)}, u32[]{:S(2)}) copy-start(f32[4096]{0:T(1024)} %copy-done.2) | copy-start | bytes 49156
  239.0 1526.0 %reduce-scatter.2.cloned.1.call-start = ((), (), s32[]{:S(2)}) async-start(), calls=%async_computation.2 | async-start | bytes 294912000 | tf_op jit(solution)/shard_map/reduce_scatter | solution.py:30
Sparse Core Ops, SparseCore 0:
  239.1 193.2 all-reduce.3
Sparse Core Ops, SparseCore 1:
  344.5 1420.5 reduce-scatter.1
where the time goes:
time: 1770 us
  waiting for transfers between devices  1380 us (78%)
  matrix products  265 us (15%)
  other arithmetic  58.1 us (3%)
  blocking collectives  51.1 us (3%)
  between operations  18 us (1%)
    reduce_scatter x1, waiting for transfers between devices, local_step(): lax.psum_scatter(w_grad_part, 'dp', scatter_dimension=0, tiled=True)  1290 us
    dot_general x1, matrix products, local_step(): lax.dot_general(normed, d_logits, (((0,), (0,)), ((), ())), preferred_ele...  105 us
    psum x1, waiting for transfers between devices, local_step(): d_normed = lax.psum(dn_part, 'tp')  88 us
    dot_general x1, matrix products, local_step(): lax.dot_general(d_logits, w_local, (((1,), (1,)), ((), ())), preferred_el...  80.4 us
    dot_general x1, matrix products, local_step(): logits = jnp.dot(normed, w_local, preferred_element_type=jnp.float32)  79.4 us
    psum x2, blocking collectives, local_step(): lax.psum((jnp.sum(mask_f32), jnp.sum(mask_f32 * (log_z - target))), 'dp')  41 us
  transfers between devices with their start and end apart: 2, of which 2 were waited for; matrix products, arithmetic and copies ran while one was open for 7% of the time, Pallas kernels for 0%

commit v1 on v0

v1 whole, which is shorter than its diff:
```python
import functools

import jax
import jax.numpy as jnp
from jax import lax
from jax.experimental import pallas as pl
from jax.experimental.pallas import tpu as pltpu
from jax.sharding import PartitionSpec as P

NORM_EPS = 1e-5
F32, BF16, I32 = jnp.float32, jnp.bfloat16, jnp.int32
VMEM_LIMIT = 64 * 1024 * 1024 - 64 * 1024
LANES = 128
ROWS = 8
NT = (((1,), (1,)), ((), ()))


def call(body, **kw):
    cost = kw.pop("cost")
    return pl.pallas_call(body, compiler_params=pltpu.CompilerParams(vmem_limit_bytes=VMEM_LIMIT), cost_estimate=pl.CostEstimate(flops=cost[0], bytes_accessed=cost[1], transcendentals=0), **kw)


def whole(shape):
    return pl.BlockSpec(shape, lambda *_: (0,) * len(shape))


def columns(rows):
    return jnp.transpose(jnp.concatenate([rows] * (LANES // ROWS), axis=0))


def softmax_grad(z, cols, first):
    hot = lax.broadcasted_iota(I32, z.shape, 1) + first == cols[:, 2:3].astype(I32)
    return ((jnp.exp(z - cols[:, 0:1]) - hot.astype(F32)) * cols[:, 1:2]).astype(BF16)


def token_columns(picked, aux_own, aux_x, aux_y, aux_d):
    count = aux_own[3:4, 0:1] + aux_x[3:4, 0:1] + aux_y[3:4, 0:1] + aux_d[3:4, 0:1]
    row = lax.broadcasted_iota(I32, picked.shape, 0)
    return columns(jnp.where(row == 1, picked / count, picked))


def prep_body(x_ref, gain_ref, hat_ref, n_ref, inv_ref):
    x = x_ref[...].astype(F32)
    inv = lax.rsqrt(jnp.mean(x * x, axis=-1, keepdims=True) + NORM_EPS)
    hat = x * inv
    hat_ref[...] = hat
    n_ref[...] = (hat * gain_ref[...]).astype(BF16)
    inv_ref[...] = inv


def prep_half(x, gain, part, block=128):
    t, h = x.shape
    half = t // 2
    steps = half // block
    return call(
        prep_body,
        grid=(steps,),
        in_specs=[pl.BlockSpec((block, h), lambda j: (j + part * steps, 0)), whole((1, h))],
        out_specs=[pl.BlockSpec((block, h), lambda j: (j, 0)), pl.BlockSpec((block, h), lambda j: (j, 0)), pl.BlockSpec((block, 1), lambda j: (j, 0))],
        out_shape=[jax.ShapeDtypeStruct((half, h), F32), jax.ShapeDtypeStruct((half, h), BF16), jax.ShapeDtypeStruct((half, 1), F32)],
        cost=(8 * half * h, 8 * half * h),
    )(x, gain)


def own_body(n0_ref, n1_ref, w_ref, lab_ref, z_ref, st_ref, n_sc, lab_sc, m_sc, s_sc, t_sc, *, tile, chunk, vocab):
    j = pl.program_id(0)
    half = n0_ref.shape[0]

    @pl.when(j == 0)
    def _():
        n_sc[:half, :] = n0_ref[...]
        n_sc[half:, :] = n1_ref[...]
        lab_sc[...] = columns(lab_ref[...])
        m_sc[...] = jnp.full(m_sc.shape, -jnp.inf, F32)
        s_sc[...] = jnp.zeros(s_sc.shape, F32)
        t_sc[...] = jnp.zeros(t_sc.shape, F32)

    for c in range(0, tile, chunk):
        z = jnp.dot(n_sc[...], w_ref[:, c:c + chunk], preferred_element_type=F32)
        z_ref[:, c:c + chunk] = z
        lab = lab_sc[:, 0:1].astype(I32) - (j * tile + c)
        parts = []
        for k in range(0, chunk, LANES):
            zk = z[:, k:k + LANES]
            hot = lax.broadcasted_iota(I32, zk.shape, 1) + k == lab
            if c + k >= vocab % tile:
                inside = j * tile + c + k < vocab
                hot = hot & inside
                zk = jnp.where(inside, zk, -jnp.inf)
            t_sc[...] += jnp.where(hot, zk, 0.0)
            parts.append(zk)
        old = m_sc[...]
        top = functools.reduce(jnp.maximum, parts, old)
        s_sc[...] = functools.reduce(jnp.add, [jnp.exp(zk - top) for zk in parts], s_sc[...] * jnp.exp(old - top))
        m_sc[...] = top

    @pl.when(j == pl.num_programs(0) - 1)
    def _():
        m = jnp.max(m_sc[...], axis=1, keepdims=True)
        s = jnp.sum(s_sc[...] * jnp.exp(m_sc[...] - m), axis=1, keepdims=True)
        t = jnp.sum(t_sc[...], axis=1, keepdims=True)
        lane = lax.broadcasted_iota(I32, (m.shape[0], LANES), 1)
        st_ref[...] = jnp.transpose(jnp.where(lane == 0, m, jnp.where(lane == 1, s, t)))[:ROWS, :]


def own_logits(n0, n1, w, lab, tile=768, chunk=256):
    half, h = n0.shape
    t, v = 2 * half, w.shape[1]
    return call(
        functools.partial(own_body, tile=tile, chunk=chunk, vocab=v),
        grid=(pl.cdiv(v, tile),),
        in_specs=[whole((half, h)), whole((half, h)), pl.BlockSpec((h, tile), lambda j: (0, j)), whole((ROWS, t))],
        out_specs=[pl.BlockSpec((t, tile), lambda j: (0, j)), whole((ROWS, t))],
        out_shape=[jax.ShapeDtypeStruct((t, v), F32), jax.ShapeDtypeStruct((ROWS, t), F32)],
        scratch_shapes=[pltpu.VMEM((t, h), BF16)] + [pltpu.VMEM((t, LANES), F32)] * 4,
        cost=(2 * t * h * v, 2 * h * v + 4 * t * v),
    )(n0, n1, w, lab)


def combine_body(tp_ref, mine_ref, other_ref, info_ref, aux_ref):
    first = tp_ref[0] == 0
    mine, other, info = mine_ref[...], other_ref[...], info_ref[...]
    a, b = jnp.where(first, mine, other), jnp.where(first, other, mine)
    top = jnp.maximum(a[0:1], b[0:1])
    log_z = top + jnp.log(a[1:2] * jnp.exp(a[0:1] - top) + b[1:2] * jnp.exp(b[0:1] - top))
    mask, label, count = info[1:2], info[0:1], info[2:3]
    lost = jnp.sum(mask * (log_z - (a[2:3] + b[2:3])), axis=1, keepdims=True)
    row = lax.broadcasted_iota(I32, aux_ref.shape, 0)
    out = jnp.where(row == 0, log_z, jnp.where(row == 1, mask, jnp.where(row == 2, label, jnp.where(row == 3, count, lost))))
    aux_ref[...] = out


def combine(tp, mine, other, info):
    shape = mine.shape
    return call(
        combine_body,
        in_specs=[pl.BlockSpec(memory_space=pltpu.SMEM)] + [whole(shape)] * 3,
        out_specs=whole(shape),
        out_shape=jax.ShapeDtypeStruct(shape, F32),
        cost=(1000, 1000),
    )(tp, mine, other, info)


def back_body(z_ref, w_ref, own_ref, ax_ref, ay_ref, ad_ref, g_ref, dn_ref, cols, *, tile, vocab, rows):
    j = pl.program_id(0)
    last = pl.num_programs(0) - 1

    @pl.when(j == 0)
    def _():
        cols[...] = token_columns(own_ref[...], own_ref, ax_ref, ay_ref, ad_ref)
        dn_ref[...] = jnp.zeros(dn_ref.shape, F32)

    def step(width):
        g = softmax_grad(z_ref[:, :width], cols, j * tile)
        g_ref[:, :width] = g
        for c in range(0, w_ref.shape[0], rows):
            dn_ref[:, c:c + rows] += lax.dot_general(g, w_ref[c:c + rows, :width], NT, preferred_element_type=F32)

    @pl.when(j < last)
    def _():
        step(tile)

    @pl.when(j == last)
    def _():
        step(vocab - (pl.cdiv(vocab, tile) - 1) * tile)


def own_grad(z, w, auxes, slots, tile=1024, rows=1024):
    t, v = z.shape
    h = w.shape[0]
    return call(
        functools.partial(back_body, tile=tile, vocab=v, rows=rows),
        grid=(pl.cdiv(v, tile),),
        in_specs=[pl.BlockSpec((t, tile), lambda j: (0, j)), pl.BlockSpec((h, tile), lambda j: (0, j))] + [whole((ROWS, t))] * 4,
        out_specs=[pl.BlockSpec((t, tile), lambda j: (0, j)), whole((t, h))],
        out_shape=[jax.ShapeDtypeStruct((slots * t, v), BF16), jax.ShapeDtypeStruct((t, h), F32)],
        scratch_shapes=[pltpu.VMEM((t, LANES), F32)],
        cost=(2 * t * h * v, 2 * h * v + 6 * t * v),
    )(z, w, *auxes)


def remote_body(h0_ref, h1_ref, gain_ref, w_ref, own_ref, ax_ref, ay_ref, ad_ref, _, g_ref, n_ref, cols, *, tile, chunk, pick):
    half = h0_ref.shape[0]

    @pl.when(pl.program_id(0) == 0)
    def _():
        n_ref[:half, :] = (h0_ref[...] * gain_ref[...]).astype(BF16)
        n_ref[half:, :] = (h1_ref[...] * gain_ref[...]).astype(BF16)
        from_other = (ax_ref, ay_ref, ad_ref)
        lane = lax.broadcasted_iota(I32, ax_ref.shape, 1)
        (a, a_half), (b, _) = pick
        picked = jnp.where((lane < half) == (a_half == 0), from_other[a][...], from_other[b][...])
        if a_half != 0:
            picked = pltpu.roll(picked, half, 1)
        cols[...] = token_columns(picked, own_ref, ax_ref, ay_ref, ad_ref)

    for c in range(0, tile, chunk):
        z = jnp.dot(n_ref[...], w_ref[:, c:c + chunk], preferred_element_type=F32)
        g_ref[:, c:c + chunk] = softmax_grad(z, cols, pl.program_id(0) * tile + c)


def remote_grad(h0, h1, gain, w, auxes, g_all, slot, pick, tile=768, chunk=256):
    half, h = h0.shape
    t, v = 2 * half, w.shape[1]
    return call(
        functools.partial(remote_body, tile=tile, chunk=chunk, pick=pick),
        grid=(pl.cdiv(v, tile),),
        in_specs=[whole((half, h)), whole((half, h)), whole((1, h)), pl.BlockSpec((h, tile), lambda j: (0, j))] + [whole((ROWS, t))] * 4 + [pl.BlockSpec(memory_space=pl.ANY)],
        out_specs=[pl.BlockSpec((t, tile), lambda j: (slot, j)), whole((t, h))],
        out_shape=[jax.ShapeDtypeStruct(g_all.shape, BF16), jax.ShapeDtypeStruct((t, h), BF16)],
        scratch_shapes=[pltpu.VMEM((t, LANES), F32)],
        input_output_aliases={8: 0},
        cost=(2 * t * h * v, 2 * h * v + 2 * t * v),
    )(h0, h1, gain, w, *auxes, g_all)


def wgrad_body(at_ref, *refs, tile, chunk, pieces, with_add):
    n_refs, g_ref, rest, nt = refs[:pieces], refs[pieces], refs[pieces + 1:-1], refs[-1]
    out_ref = rest[-1]

    @pl.when(pl.program_id(0) == 0)
    def _():
        first = 0
        for ref in n_refs:
            size = ref.shape[0]
            nt[:, first:first + size] = jnp.transpose(ref[...].astype(F32)).astype(BF16)
            first += size

    for c in range(0, tile, chunk):
        part = jnp.dot(nt[...], g_ref[:, c:c + chunk], preferred_element_type=F32)
        out_ref[:, c:c + chunk] = part + rest[0][:, c:c + chunk] if with_add else part


def weight_grad(at, ns, g, first, tiles, add=None, into=None, tile=1792, chunk=256):
    k, v = g.shape
    r = k // 4
    width = min(v - first * tile, tiles * tile)
    ins, aliases = [*ns, g], {}
    specs = [pl.BlockSpec((n.shape[0], r), lambda j, at_ref: (0, at_ref[0])) for n in ns] + [pl.BlockSpec((k, tile), lambda j, at_ref: (0, j + first))]
    out_spec, out_shape = pl.BlockSpec((r, tile), lambda j, at_ref: (0, j)), (r, width)
    if add is not None:
        ins.append(add)
        specs.append(pl.BlockSpec((r, tile), lambda j, at_ref: (0, j)))
        out_spec, out_shape = pl.BlockSpec((r, tile), lambda j, at_ref: (0, j + first)), (r, v)
        if into is not None:
            ins.append(into)
            specs.append(pl.BlockSpec(memory_space=pl.ANY))
            aliases = {len(ins): 0}
    return call(
        functools.partial(wgrad_body, tile=tile, chunk=chunk, pieces=len(ns), with_add=add is not None),
        grid_spec=pltpu.PrefetchScalarGridSpec(num_scalar_prefetch=1, grid=(tiles,), in_specs=specs, out_specs=out_spec, scratch_shapes=[pltpu.VMEM((r, k), BF16)]),
        out_shape=jax.ShapeDtypeStruct(out_shape, F32),
        input_output_aliases=aliases,
        cost=(2 * r * k * width, 2 * k * width + 4 * r * width),
    )(at, *ins)


def final_body(x_ref, inv0_ref, inv1_ref, gain_ref, mine_ref, other_ref, dh_ref, gam_ref):
    j = pl.program_id(0)
    first = j < pl.num_programs(0) // 2
    inv = jnp.where(first, inv0_ref[...], inv1_ref[...])
    hat = x_ref[...].astype(F32) * inv
    dn = mine_ref[...] + other_ref[...]
    prod = dn * hat

    @pl.when(j == 0)
    def _():
        gam_ref[...] = jnp.zeros(gam_ref.shape, F32)

    gam_ref[...] += jnp.sum(prod.reshape(-1, ROWS, prod.shape[1]), axis=0)
    d_hat = dn * gain_ref[...]
    dh_ref[...] = (inv * (d_hat - hat * jnp.mean(d_hat * hat, axis=-1, keepdims=True))).astype(BF16)


def final(x, inv0, inv1, gain, mine, other, block=64):
    t, h = x.shape
    steps = t // block
    half = steps // 2
    rows = pl.BlockSpec((block, h), lambda j: (j, 0))
    return call(
        final_body,
        grid=(steps,),
        in_specs=[rows, pl.BlockSpec((block, 1), lambda j: (jnp.minimum(j, half - 1), 0)), pl.BlockSpec((block, 1), lambda j: (jnp.maximum(j - half, 0), 0)), whole((1, h)), rows, rows],
        out_specs=[rows, whole((ROWS, h))],
        out_shape=[jax.ShapeDtypeStruct((t, h), BF16), jax.ShapeDtypeStruct((ROWS, h), F32)],
        cost=(10 * t * h, 12 * t * h),
    )(x, inv0, inv1, gain, mine, other)


def solution(mesh):
    n_dp = mesh.shape["dp"]

    def swap(v, bits):
        return lax.ppermute(v, "dp", [(i, i ^ bits) for i in range(n_dp)])

    def swap_tp(v):
        return lax.ppermute(v, "tp", [(0, 1), (1, 0)])

    def step(hidden_in, labels, loss_mask, norm_gamma, w_local):
        tp, dp = lax.axis_index("tp"), lax.axis_index("dp")
        gain = norm_gamma.astype(F32)[None, :]
        mask = loss_mask.astype(F32)
        count = jnp.sum(mask).reshape(1, 1)
        count = count + swap(count, 1)
        local = (labels - tp * w_local.shape[1]).astype(F32)
        info = jnp.concatenate([local[None], mask[None], jnp.broadcast_to(count, (ROWS - 2, mask.shape[0]))], axis=0)

        low, n_low, inv_low = prep_half(hidden_in, gain, 0)
        high, n_high, inv_high = prep_half(hidden_in, gain, 1)
        x_low, y_high = swap(low, 2), swap(high, 4)
        lab_rows = jnp.broadcast_to(local[None], (ROWS, mask.shape[0]))
        logits, stats = own_logits(n_low, n_high, w_local, lab_rows)
        aux = combine(tp.reshape(1), stats, swap_tp(stats), info)
        aux_x, aux_y, aux_d = swap(aux, 2), swap(aux, 4), swap(aux, 6)
        auxes = (aux, aux_x, aux_y, aux_d)
        x_low, y_high, low, high, auxes = lax.optimization_barrier((x_low, y_high, low, high, auxes))
        d_low, d_high = swap(x_low, 4), swap(y_high, 2)
        x_high, y_low = swap(high, 2), swap(low, 4)

        g_all, dn_mine = own_grad(logits, w_local, auxes, 4)
        dn_other = swap_tp(dn_mine)
        ns = [n_low, n_high]
        for slot, h0, h1, pick in ((1, x_low, y_high, ((0, 0), (1, 1))), (2, d_low, d_high, ((2, 0), (2, 1))), (3, x_high, y_low, ((0, 1), (1, 0)))):
            g_all, n = remote_grad(h0, h1, gain, w_local, auxes, g_all, slot, pick)
            ns.append(n)

        own_at, other_at = dp.reshape(1), (dp ^ 1).reshape(1)
        p1 = swap(weight_grad(other_at, ns, g_all, 0, 5), 1)
        p2 = swap(weight_grad(other_at, ns, g_all, 5, 4), 1)
        d_w_out = weight_grad(own_at, ns, g_all, 0, 5, add=p1)
        d_w_out = weight_grad(own_at, ns, g_all, 5, 4, add=p2, into=d_w_out)

        d_hidden, gam = final(hidden_in, inv_low, inv_high, gain, dn_mine, dn_other)
        d_gamma = jnp.sum(gam, axis=0)
        for bit in (1, 2, 4):
            d_gamma = d_gamma + swap(d_gamma, bit)
        total = (aux[3, 0] + aux_x[3, 0]) + (aux_y[3, 0] + aux_d[3, 0])
        lost = ((aux[4, 0] + aux_x[4, 0]) + (aux_y[4, 0] + aux_d[4, 0])).reshape(1)
        loss = (lost + swap(lost, 1))[0] / total
        return (loss, d_hidden, d_w_out, d_gamma)

    return jax.shard_map(step, mesh=mesh, in_specs=(P("dp", None), P("dp"), P("dp"), P(), P(None, "tp")), out_specs=(P(), P("dp", None), P("dp", "tp"), P()), check_vma=False)
```

time: 1770 us -> 784 us (0.44)
  waiting for transfers between devices: 1380 us -> 185 us
  Pallas kernels: 0 us -> 552 us
  matrix products: 265 us -> 0 us
  other arithmetic: 58.1 us -> 6.9 us
  blocking collectives: 51.1 us -> 0 us
  starting transfers between devices: 0.08 us -> 18.6 us
    reduce_scatter x1 -> x0, waiting for transfers between devices: 1290 us -> none  [local_step(): lax.psum_scatter(w_grad_part, 'dp', scatter_dimension=0, tiled=True)]
    pallas_call x0 -> x13, Pallas kernels: none -> 552 us  [the longest x3 249 us: remote_grad(): call(functools.partial(remote_body, tile=tile, chunk=chunk, pick=pick), g...]
    dot_general x3 -> x0, matrix products: 265 us -> none  [the longest x1 105 us: local_step(): lax.dot_general(normed, d_logits, (((0,), (0,)), ((), ())), preferred_ele...]
    ppermute x0 -> x18, waiting for transfers between devices: none -> 185 us  [the longest x2 181 us: swap_tp(): return lax.ppermute(v, 'tp', [(0, 1), (1, 0)])]
    psum x1 -> x0, waiting for transfers between devices: 88 us -> none  [local_step(): d_normed = lax.psum(dn_part, 'tp')]
    psum x3 -> x0, blocking collectives: 46.1 us -> none  [the longest x2 41 us: local_step(): lax.psum((jnp.sum(mask_f32), jnp.sum(mask_f32 * (log_z - target))), 'dp')]
    reduce_sum x4 -> x2, other arithmetic: 27 us -> 2.25 us  [the longest x1 1.31 us: step(): count = jnp.sum(mask).reshape(1, 1)]
    dot_general x1 -> x0, other arithmetic: 20.5 us -> none  [local_step(): lax.dot_general(d_logits, w_local, (((1,), (1,)), ((), ())), preferred_el...]
  transfers between devices with their start and end apart: 2 -> 18, of which waited for: 2 -> 6; matrix products, arithmetic and copies ran while one was open for 7% -> 1% of each run, Pallas kernels for 0% -> 53%
where the time goes in v1:
time: 784 us; the launch traced here: 778 us
  Pallas kernels  552 us (70%)
  waiting for transfers between devices  185 us (24%)
  starting transfers between devices  18.6 us (2%)
  between operations  8.81 us (1%)
    pallas_call x3, Pallas kernels, remote_grad(): call(functools.partial(remote_body, tile=tile, chunk=chunk, pick=pick), g...  249 us
    ppermute x2, waiting for transfers between devices, swap_tp(): return lax.ppermute(v, 'tp', [(0, 1), (1, 0)])  181 us
    pallas_call x4, Pallas kernels, weight_grad(): call(functools.partial(wgrad_body, tile=tile, chunk=chunk, pieces=len(ns)...  107 us
    pallas_call x1, Pallas kernels, own_grad(): call(functools.partial(back_body, tile=tile, vocab=v, rows=rows), grid=(p...  87.8 us
    pallas_call x1, Pallas kernels, own_logits(): call(functools.partial(own_body, tile=tile, chunk=chunk, vocab=v), grid=(...  85.2 us
    ppermute x16, starting transfers between devices, swap(): return lax.ppermute(v, 'dp', [(i, i ^ bits) for i in range(n_dp)])  17 us
  transfers between devices with their start and end apart: 18, of which 6 were waited for; matrix products, arithmetic and copies ran while one was open for 1% of the time, Pallas kernels for 53%

profile of v1, /device:TPU:0, one launch (start us, length us, event | category | flops | bytes accessed | tf_op | source)
XLA Modules:
  0.0 778.5 jit_solution(4670345438695024255)
XLA Ops:
  0.6 1.3 broadcast_in_dim.31
  1.9 4.5 shard_map.84
  6.4 3.2 collective-permute-start.6
  9.6 4.4 shard_map.85
  14.0 1.5 collective-permute-start.7
  15.5 0.7 subtract_convert_fusion
  16.2 0.6 copy-done
  16.8 0.6 broadcast_in_dim.26.lab_ref
  17.4 85.2 %shard_map.86 = (f32[512,16000]{1,0:T(8,128)}, f32[8,512]{1,0:T(8,128)}) custom-call(bf16[256,4096]{1,0:T(8,128)(2,1)} %get-tuple-element.30.n0_ref.refs_0_, bf16[256,4096]{1,0:T(8,128)(2,1)} %get-tuple-element.31.n1_ref.refs_1_, bf16[4096,16000]{1,0:T(8,128)(2,1)} %w_ref.9, f32[8,512]{1,0:T(8,128)} %broadcast_in_dim.26.lab_ref), custom_call_target="tpu_custom_call" | custom-call | flops 67108864000 | bytes 163840000 | tf_op jit(solution)/shard_map/pallas_call | solution.py:109
  102.6 1.6 collective-permute-start
  104.1 1.3 convert_reduce_fusion
  105.5 0.7 convert_element_type.8
  106.1 0.5 collective-permute-done.1
  107.9 0.1 pad.2.clone
  108.0 1.4 maximum_maximum_fusion.info_ref
  109.4 1.5 shard_map.87.own_ref
  110.8 0.5 collective-permute-start.2
  111.4 0.5 collective-permute-start.3
  111.9 2.5 collective-permute-start.4
  114.3 0.6 collective-permute-done.2.ax_ref
  114.9 0.7 collective-permute-done.3.ay_ref
  115.6 1.2 collective-permute-done.4.ad_ref
  116.8 1.5 collective-permute-start.10
  118.3 1.5 collective-permute-start.9
  119.9 0.5 collective-permute-start.11
  120.4 0.5 collective-permute-start.12
  120.9 87.8 %shard_map.88 = (bf16[2048,16000]{1,0:T(8,128)(2,1)}, f32[512,4096]{1,0:T(8,128)}) custom-call(f32[512,16000]{1,0:T(8,128)} %get-tuple-element.35.z_ref, bf16[4096,16000]{1,0:T(8,128)(2,1)} %w_ref.9, f32[8,512]{1,0:T(8,128)} %shard_map.87.own_ref, f32[8,512]{1,0:T(8,128)} %collective-permute-done.2.ax_ref, f32[8,512]{1,0:T(8,128)} %collective-permute-done.3.ay_ref, ...), custom_call_target="tpu_custom_call" | custom-call | flops 67108864000 | bytes 180224000 | tf_op jit(solution)/shard_map/pallas_call | solution.py:171
  208.7 82.7 %shard_map.90 = (bf16[2048,16000]{1,0:T(8,128)(2,1)}, bf16[512,4096]{1,0:T(8,128)(2,1)}) custom-call(f32[256,4096]{1,0:T(8,128)} %collective-permute-done.6.h0_ref, f32[256,4096]{1,0:T(8,128)} %collective-permute-done.7.h1_ref, f32[1,4096]{1,0:T(1,128)} %bitcast.13, bf16[4096,16000]{1,0:T(8,128)(2,1)} %w_ref.9, ...), custom_call_target="tpu_custom_call", output_to_operand_aliasing={{0}: (8, {})} | custom-call | flops 67108864000 | bytes 147456000 | tf_op jit(solution)/shard_map/pallas_call | solution.py:205
  291.5 83.1 %shard_map.91 = (bf16[2048,16000]{1,0:T(8,128)(2,1)}, bf16[512,4096]{1,0:T(8,128)(2,1)}) custom-call(f32[256,4096]{1,0:T(8,128)} %collective-permute-done.9.h0_ref, f32[256,4096]{1,0:T(8,128)} %collective-permute-done.10.h1_ref, f32[1,4096]{1,0:T(1,128)} %bitcast.14, bf16[4096,16000]{1,0:T(8,128)(2,1)} %w_ref.9, ...), custom_call_target="tpu_custom_call", output_to_operand_aliasing={{0}: (8, {})} | custom-call | flops 67108864000 | bytes 147456000 | tf_op jit(solution)/shard_map/pallas_call | solution.py:205
  374.6 82.8 %shard_map.92 = (bf16[2048,16000]{1,0:T(8,128)(2,1)}, bf16[512,4096]{1,0:T(8,128)(2,1)}) custom-call(f32[256,4096]{1,0:T(8,128)} %collective-permute-done.11.h0_ref, f32[256,4096]{1,0:T(8,128)} %collective-permute-done.12.h1_ref, f32[1,4096]{1,0:T(1,128)} %bitcast.15, bf16[4096,16000]{1,0:T(8,128)(2,1)} %w_ref.9, ...), custom_call_target="tpu_custom_call", output_to_operand_aliasing={{0}: (8, {})} | custom-call | flops 67108864000 | bytes 147456000 | tf_op jit(solution)/shard_map/pallas_call | solution.py:205
  457.4 26.9 %shard_map.94 = f32[512,8960]{1,0:T(8,128)} custom-call(s32[1]{0:T(128)} %bitcast.10.at_ref, bf16[256,4096]{1,0:T(8,128)(2,1)} %get-tuple-element.30.n0_ref.refs_0_, bf16[256,4096]{1,0:T(8,128)(2,1)} %get-tuple-element.31.n1_ref.refs_1_, bf16[512,4096]{1,0:T(8,128)(2,1)} %get-tuple-element.47.refs_2_, bf16[512,4096]{1,0:T(8,128)(2,1)} %get-tuple-element.49.refs_3_, ...), custom_call_target="tpu_custom_call" | custom-call | flops 18790481920 | bytes 55050240 | tf_op jit(solution)/shard_map/pallas_call | solution.py:249
  484.3 22.7 %shard_map.93 = f32[512,7040]{1,0:T(8,128)} custom-call(s32[1]{0:T(128)} %bitcast.10.at_ref, bf16[256,4096]{1,0:T(8,128)(2,1)} %get-tuple-element.30.n0_ref.refs_0_, bf16[256,4096]{1,0:T(8,128)(2,1)} %get-tuple-element.31.n1_ref.refs_1_, bf16[512,4096]{1,0:T(8,128)(2,1)} %get-tuple-element.47.refs_2_, bf16[512,4096]{1,0:T(8,128)(2,1)} %get-tuple-element.49.refs_3_, ...), custom_call_target="tpu_custom_call" | custom-call | flops 14763950080 | bytes 43253760 | tf_op jit(solution)/shard_map/pallas_call | solution.py:249
  507.0 0.5 collective-permute-start.13
  507.5 1.3 fusion.3
  508.8 181.4 %collective-permute-done.8.other_ref = f32[512,4096]{1,0:T(8,128)} collective-permute-done((f32[512,4096]{1,0:T(8,128)}, f32[512,4096]{1,0:T(8,128)}, u32[]{:S(2)}, u32[]{:S(2)}) %collective-permute-start.8) | collective-permute-done | bytes 8388640 | tf_op jit(solution)/shard_map/ppermute | solution.py:297
  690.2 13.0 %shard_map.89 = (bf16[512,4096]{1,0:T(8,128)(2,1)}, f32[8,4096]{1,0:T(8,128)}) custom-call(bf16[512,4096]{1,0:T(8,128)(2,1)} %x_ref.5, f32[256,1]{1,0:T(8,128)} %get-tuple-element.33.inv0_ref, f32[256,1]{1,0:T(8,128)} %get-tuple-element.34.inv1_ref, f32[1,4096]{1,0:T(1,128)} %bitcast.16, f32[512,4096]{1,0:T(8,128)} %get-tuple-element.42.mine_ref, ...), custom_call_target="tpu_custom_call" | custom-call | flops 20971520 | bytes 25165824 | tf_op jit(solution)/shard_map/pallas_call | solution.py:280
  703.2 0.9 reduce_sum.19
  704.1 0.0 collective-permute-start.15
  704.2 1.3 fusion
  705.5 1.6 collective-permute-start.16
  707.1 1.3 fusion.1
  708.4 0.9 collective-permute-done.16
  709.3 1.6 collective-permute-start.17
  710.8 1.3 fusion.2
  714.5 1.0 collective-permute-start.5
  718.6 0.6 add.52
  719.3 32.3 %shard_map.95.refs_7_ = f32[512,16000]{1,0:T(8,128)} custom-call(s32[1]{0:T(128)} %bitcast.9.at_ref, bf16[256,4096]{1,0:T(8,128)(2,1)} %get-tuple-element.30.n0_ref.refs_0_, bf16[256,4096]{1,0:T(8,128)(2,1)} %get-tuple-element.31.n1_ref.refs_1_, bf16[512,4096]{1,0:T(8,128)(2,1)} %get-tuple-element.47.refs_2_, bf16[512,4096]{1,0:T(8,128)(2,1)} %get-tuple-element.49.refs_3_, ...), custom_call_target="tpu_custom_call" | custom-call | flops 18790481920 | bytes 55050240 | tf_op jit(solution)/shard_map/pallas_call | solution.py:249
  751.5 25.6 %shard_map.96 = f32[512,16000]{1,0:T(8,128)} custom-call(s32[1]{0:T(128)} %bitcast.9.at_ref, bf16[256,4096]{1,0:T(8,128)(2,1)} %get-tuple-element.30.n0_ref.refs_0_, bf16[256,4096]{1,0:T(8,128)(2,1)} %get-tuple-element.31.n1_ref.refs_1_, bf16[512,4096]{1,0:T(8,128)(2,1)} %get-tuple-element.47.refs_2_, ...), custom_call_target="tpu_custom_call", output_to_operand_aliasing={{}: (8, {})} | custom-call | flops 14763950080 | bytes 43253760 | tf_op jit(solution)/shard_map/pallas_call | solution.py:249
  (19 shorter events, 0.1 us)
Async XLA Ops:
  6.4 110.4 %collective-permute-start.6 = (f32[256,4096]{1,0:T(8,128)}, f32[256,4096]{1,0:T(8,128)}, u32[]{:S(2)}, u32[]{:S(2)}) collective-permute-start(f32[256,4096]{1,0:T(8,128)} %get-tuple-element.51), channel_id=1, source_target_pairs={{0,2},{1,3},{2,0},{3,1},{4,6},{5,7},{6,4},{7,5},{8,10},{9,11},{10,... | collective-permute-start | bytes 12582920 | tf_op jit(solution)/shard_map/ppermute | solution.py:294
  14.0 102.9 %collective-permute-start.7 = (f32[256,4096]{1,0:T(8,128)}, f32[256,4096]{1,0:T(8,128)}, u32[]{:S(2)}, u32[]{:S(2)}) collective-permute-start(f32[256,4096]{1,0:T(8,128)} %get-tuple-element.50), channel_id=1, source_target_pairs={{0,4},{1,5},{2,6},{3,7},{4,0},{5,1},{6,2},{7,3},{8,12},{9,13},{10,... | collective-permute-start | bytes 12582920 | tf_op jit(solution)/shard_map/ppermute | solution.py:294
  16.2 0.6 copy-start
  102.6 6.8 collective-permute-start
  105.5 1.2 collective-permute-start.1
  110.8 4.1 collective-permute-start.2
  111.4 4.2 collective-permute-start.3
  111.9 5.0 collective-permute-start.4
  116.8 174.6 %collective-permute-start.10 = (f32[256,4096]{1,0:T(8,128)}, f32[256,4096]{1,0:T(8,128)}, u32[]{:S(2)}, u32[]{:S(2)}) collective-permute-start(f32[256,4096]{1,0:T(8,128)} %collective-permute-done.7.h1_ref), channel_id=1, source_target_pairs={{0,2},{1,3},{2,0},{3,1},{4,6},{5,7},{6,4},{7,5},{8,10},{9,11},{10,... | collective-permute-start | bytes 12582920 | tf_op jit(solution)/shard_map/ppermute | solution.py:294
  118.3 173.1 %collective-permute-start.9 = (f32[256,4096]{1,0:T(8,128)}, f32[256,4096]{1,0:T(8,128)}, u32[]{:S(2)}, u32[]{:S(2)}) collective-permute-start(f32[256,4096]{1,0:T(8,128)} %collective-permute-done.6.h0_ref), channel_id=1, source_target_pairs={{0,4},{1,5},{2,6},{3,7},{4,0},{5,1},{6,2},{7,3},{8,12},{9,13},{10,... | collective-permute-start | bytes 12582920 | tf_op jit(solution)/shard_map/ppermute | solution.py:294
  119.9 254.8 %collective-permute-start.11 = (f32[256,4096]{1,0:T(8,128)}, f32[256,4096]{1,0:T(8,128)}, u32[]{:S(2)}, u32[]{:S(2)}) collective-permute-start(f32[256,4096]{1,0:T(8,128)} %get-tuple-element.50), channel_id=1, source_target_pairs={{0,2},{1,3},{2,0},{3,1},{4,6},{5,7},{6,4},{7,5},{8,10},{9,11},{10,... | collective-permute-start | bytes 12582920 | tf_op jit(solution)/shard_map/ppermute | solution.py:294
  120.4 254.2 %collective-permute-start.12 = (f32[256,4096]{1,0:T(8,128)}, f32[256,4096]{1,0:T(8,128)}, u32[]{:S(2)}, u32[]{:S(2)}) collective-permute-start(f32[256,4096]{1,0:T(8,128)} %get-tuple-element.51), channel_id=1, source_target_pairs={{0,4},{1,5},{2,6},{3,7},{4,0},{5,1},{6,2},{7,3},{8,12},{9,13},{10,... | collective-permute-start | bytes 12582920 | tf_op jit(solution)/shard_map/ppermute | solution.py:294
  484.3 235.0 %collective-permute-start.14 = (f32[512,8960]{1,0:T(8,128)}, f32[512,8960]{1,0:T(8,128)}, u32[]{:S(2)}, u32[]{:S(2)}) collective-permute-start(f32[512,8960]{1,0:T(8,128)} %shard_map.94), channel_id=1, source_target_pairs={{0,1},{1,0},{2,3},{3,2},{4,5},{5,4},{6,7},{7,6},{8,9},{9,8},{10,11... | collective-permute-start | bytes 55050248 | tf_op jit(solution)/shard_map/ppermute | solution.py:294
  507.0 244.5 %collective-permute-start.13 = (f32[512,7040]{1,0:T(8,128)}, f32[512,7040]{1,0:T(8,128)}, u32[]{:S(2)}, u32[]{:S(2)}) collective-permute-start(f32[512,7040]{1,0:T(8,128)} %shard_map.93), channel_id=1, source_target_pairs={{0,1},{1,0},{2,3},{3,2},{4,5},{5,4},{6,7},{7,6},{8,9},{9,8},{10,11... | collective-permute-start | bytes 43253768 | tf_op jit(solution)/shard_map/ppermute | solution.py:294
  507.5 182.7 %collective-permute-start.8 = (f32[512,4096]{1,0:T(8,128)}, f32[512,4096]{1,0:T(8,128)}, u32[]{:S(2)}, u32[]{:S(2)}) collective-permute-start(f32[512,4096]{1,0:T(8,128)} %get-tuple-element.42.mine_ref), channel_id=1, source_target_pairs={{0,8},{8,0},{1,9},{9,1},{2,10},{10,2},{3,11},{11,3},{4,12},{12,4},... | collective-permute-start | bytes 25165832 | tf_op jit(solution)/shard_map/ppermute | solution.py:297
  704.1 1.4 collective-permute-start.15
  705.5 3.8 collective-permute-start.16
  709.3 9.4 %collective-permute-start.17 = (f32[4096]{0:T(1024)S(1)}, f32[4096]{0:T(1024)S(1)}, u32[]{:S(2)}, u32[]{:S(2)}) collective-permute-start(f32[4096]{0:T(1024)S(1)} %add.51), channel_id=1, source_target_pairs={{0,4},{1,5},{2,6},{3,7},{4,0},{5,1},{6,2},{7,3},{8,12},{9,13},{10,... | collective-permute-start | bytes 49160 | tf_op jit(solution)/shard_map/ppermute | solution.py:294
  714.5 3.5 collective-permute-start.5

commit v2 on v1

v2 whole, which is shorter than its diff:
```python
import functools

import jax
import jax.numpy as jnp
from jax import lax
from jax.experimental import pallas as pl
from jax.experimental.pallas import tpu as pltpu
from jax.sharding import PartitionSpec as P

NORM_EPS = 1e-5
F32, BF16, I32 = jnp.float32, jnp.bfloat16, jnp.int32
VMEM_LIMIT = 64 * 1024 * 1024 - 64 * 1024
LANES = 128
ROWS = 8
NT = (((1,), (1,)), ((), ()))


def call(body, **kw):
    cost = kw.pop("cost")
    return pl.pallas_call(body, compiler_params=pltpu.CompilerParams(vmem_limit_bytes=VMEM_LIMIT), cost_estimate=pl.CostEstimate(flops=cost[0], bytes_accessed=cost[1], transcendentals=0), **kw)


def whole(shape):
    return pl.BlockSpec(shape, lambda *_: (0,) * len(shape))


def columns(rows):
    return jnp.transpose(jnp.concatenate([rows] * (LANES // ROWS), axis=0))


def softmax_grad(z, cols, first):
    hot = lax.broadcasted_iota(I32, z.shape, 1) + first == cols[:, 2:3].astype(I32)
    return ((jnp.exp(z - cols[:, 0:1]) - hot.astype(F32)) * cols[:, 1:2]).astype(BF16)


def token_columns(picked, aux_own, aux_x, aux_y, aux_d):
    count = aux_own[3:4, 0:1] + aux_x[3:4, 0:1] + aux_y[3:4, 0:1] + aux_d[3:4, 0:1]
    row = lax.broadcasted_iota(I32, picked.shape, 0)
    return columns(jnp.where(row == 1, picked / count, picked))


def prep_body(tp_ref, x_ref, gain_ref, lab_ref, mask_ref, low_ref, high_ref, n_ref, inv_ref, rows_ref, cnt_ref, *, vocab):
    j = pl.program_id(0)
    half = pl.num_programs(0) // 2
    x = x_ref[...].astype(F32)
    inv = lax.rsqrt(jnp.mean(x * x, axis=-1, keepdims=True) + NORM_EPS)
    hat = x * inv
    n_ref[...] = (hat * gain_ref[...].astype(F32)).astype(BF16)
    inv_ref[...] = inv

    @pl.when(j < half)
    def _():
        low_ref[...] = hat

    @pl.when(j >= half)
    def _():
        high_ref[...] = hat

    @pl.when(j == 0)
    def _():
        mask = mask_ref[...].astype(F32)
        label = (lab_ref[...] - tp_ref[0] * vocab).astype(F32)
        row = lax.broadcasted_iota(I32, rows_ref.shape, 0)
        rows_ref[...] = jnp.where(row == 0, label, mask)
        cnt_ref[...] = jnp.broadcast_to(jnp.sum(mask, axis=1, keepdims=True), cnt_ref.shape)


def prep(tp, x, gain, labels, mask, vocab, block=128):
    t, h = x.shape
    steps = t // block
    half = steps // 2
    rows = pl.BlockSpec((block, h), lambda j: (j, 0))
    return call(
        functools.partial(prep_body, vocab=vocab),
        grid=(steps,),
        in_specs=[pl.BlockSpec(memory_space=pltpu.SMEM), rows, whole((1, h)), whole((1, t)), whole((1, t))],
        out_specs=[
            pl.BlockSpec((block, h), lambda j: (jnp.minimum(j, half - 1), 0)), pl.BlockSpec((block, h), lambda j: (jnp.maximum(j - half, 0), 0)),
            rows, pl.BlockSpec((block, 1), lambda j: (j, 0)), whole((ROWS, t)), whole((ROWS, LANES)),
        ],
        out_shape=[
            jax.ShapeDtypeStruct((t // 2, h), F32), jax.ShapeDtypeStruct((t // 2, h), F32), jax.ShapeDtypeStruct((t, h), BF16),
            jax.ShapeDtypeStruct((t, 1), F32), jax.ShapeDtypeStruct((ROWS, t), F32), jax.ShapeDtypeStruct((ROWS, LANES), F32),
        ],
        cost=(8 * t * h, 8 * t * h),
    )(tp, x, gain, labels, mask)


def own_body(n_ref, w_ref, rows_ref, z_ref, st_ref, lab_sc, m_sc, s_sc, t_sc, *, tile, block, vocab):
    j = pl.program_id(0)

    @pl.when(j == 0)
    def _():
        lab_sc[...] = columns(rows_ref[...])
        m_sc[...] = jnp.full(m_sc.shape, -jnp.inf, F32)
        s_sc[...] = jnp.zeros(s_sc.shape, F32)
        t_sc[...] = jnp.zeros(t_sc.shape, F32)

    for r in range(0, n_ref.shape[0], block):
        at = slice(r, r + block)
        z = jnp.dot(n_ref[at, :], w_ref[...], preferred_element_type=F32)
        z_ref[at, :] = z
        lab = lab_sc[at, 0:1].astype(I32) - j * tile
        parts, targets = [], []
        for k in range(0, tile, LANES):
            zk = z[:, k:k + LANES]
            hot = lax.broadcasted_iota(I32, zk.shape, 1) + k == lab
            if k >= vocab % tile:
                inside = j * tile + k < vocab
                hot = hot & inside
                zk = jnp.where(inside, zk, -jnp.inf)
            targets.append(jnp.where(hot, zk, 0.0))
            parts.append(zk)
        t_sc[at, :] += functools.reduce(jnp.add, targets)
        old = m_sc[at, :]
        top = functools.reduce(jnp.maximum, parts, old)
        s_sc[at, :] = functools.reduce(jnp.add, [jnp.exp(zk - top) for zk in parts], s_sc[at, :] * jnp.exp(old - top))
        m_sc[at, :] = top

    @pl.when(j == pl.num_programs(0) - 1)
    def _():
        m = jnp.max(m_sc[...], axis=1, keepdims=True)
        s = jnp.sum(s_sc[...] * jnp.exp(m_sc[...] - m), axis=1, keepdims=True)
        t = jnp.sum(t_sc[...], axis=1, keepdims=True)
        lane = lax.broadcasted_iota(I32, (m.shape[0], LANES), 1)
        st_ref[...] = jnp.transpose(jnp.where(lane == 0, m, jnp.where(lane == 1, s, t)))[:ROWS, :]


def own_logits(n, w, rows, tile=768, block=128):
    t, h = n.shape
    v = w.shape[1]
    return call(
        functools.partial(own_body, tile=tile, block=block, vocab=v),
        grid=(pl.cdiv(v, tile),),
        in_specs=[whole((t, h)), pl.BlockSpec((h, tile), lambda j: (0, j)), whole((ROWS, t))],
        out_specs=[pl.BlockSpec((t, tile), lambda j: (0, j)), whole((ROWS, t))],
        out_shape=[jax.ShapeDtypeStruct((t, v), F32), jax.ShapeDtypeStruct((ROWS, t), F32)],
        scratch_shapes=[pltpu.VMEM((t, LANES), F32)] * 4,
        cost=(2 * t * h * v, 2 * h * v + 4 * t * v),
    )(n, w, rows)


def combine_body(tp_ref, mine_ref, other_ref, rows_ref, cnt0_ref, cnt1_ref, aux_ref):
    first = tp_ref[0] == 0
    mine, other = mine_ref[...], other_ref[...]
    label, mask = rows_ref[0:1, :], rows_ref[1:2, :]
    a, b = jnp.where(first, mine, other), jnp.where(first, other, mine)
    top = jnp.maximum(a[0:1], b[0:1])
    log_z = top + jnp.log(a[1:2] * jnp.exp(a[0:1] - top) + b[1:2] * jnp.exp(b[0:1] - top))
    count = cnt0_ref[0:1, 0:1] + cnt1_ref[0:1, 0:1]
    lost = jnp.sum(mask * (log_z - (a[2:3] + b[2:3])), axis=1, keepdims=True)
    row = lax.broadcasted_iota(I32, aux_ref.shape, 0)
    aux_ref[...] = jnp.where(row == 0, log_z, jnp.where(row == 1, mask, jnp.where(row == 2, label, jnp.where(row == 3, count, lost))))


def combine(tp, mine, other, rows, cnt0, cnt1):
    return call(
        combine_body,
        in_specs=[pl.BlockSpec(memory_space=pltpu.SMEM)] + [whole(mine.shape)] * 3 + [whole(cnt0.shape)] * 2,
        out_specs=whole(mine.shape),
        out_shape=jax.ShapeDtypeStruct(mine.shape, F32),
        cost=(1000, 1000),
    )(tp, mine, other, rows, cnt0, cnt1)


def back_body(z_ref, w_ref, own_ref, ax_ref, ay_ref, ad_ref, g_ref, dn_ref, sum_ref, cols, *, tile, vocab, rows):
    j = pl.program_id(0)

    @pl.when(j == 0)
    def _():
        cols[...] = token_columns(own_ref[...], own_ref, ax_ref, ay_ref, ad_ref)
        dn_ref[...] = jnp.zeros(dn_ref.shape, F32)
        sums = (own_ref[...] + ax_ref[...]) + (ay_ref[...] + ad_ref[...])
        row = lax.broadcasted_iota(I32, sum_ref.shape, 0)
        sum_ref[...] = jnp.where(row == 0, sums[4:5, 0:1], sums[3:4, 0:1])

    @pl.when(j == pl.num_programs(0) - 1)
    def _():
        width = vocab - (pl.cdiv(vocab, tile) - 1) * tile
        z_ref[:, width:] = jnp.zeros((z_ref.shape[0], tile - width), F32)
        w_ref[:, width:] = jnp.zeros((w_ref.shape[0], tile - width), BF16)

    g_ref[...] = softmax_grad(z_ref[...], cols, j * tile)
    for c in range(0, w_ref.shape[0], rows):
        dn_ref[:, c:c + rows] += lax.dot_general(g_ref[...], w_ref[c:c + rows, :], NT, preferred_element_type=F32)


def own_grad(z, w, auxes, slots, tile=1024, rows=1024):
    t, v = z.shape
    h = w.shape[0]
    return call(
        functools.partial(back_body, tile=tile, vocab=v, rows=rows),
        grid=(pl.cdiv(v, tile),),
        in_specs=[pl.BlockSpec((t, tile), lambda j: (0, j)), pl.BlockSpec((h, tile), lambda j: (0, j))] + [whole((ROWS, t))] * 4,
        out_specs=[pl.BlockSpec((t, tile), lambda j: (0, j)), whole((t, h)), whole((ROWS, LANES))],
        out_shape=[jax.ShapeDtypeStruct((slots * t, v), BF16), jax.ShapeDtypeStruct((t, h), F32), jax.ShapeDtypeStruct((ROWS, LANES), F32)],
        scratch_shapes=[pltpu.VMEM((t, LANES), F32)],
        cost=(2 * t * h * v, 2 * h * v + 6 * t * v),
    )(z, w, *auxes)


def remote_body(slot_ref, h0_ref, h1_ref, gain_ref, w_ref, own_ref, ax_ref, ay_ref, ad_ref, _, g_ref, n_ref, cols, *, tile, chunk):
    half = h0_ref.shape[0]

    @pl.when(pl.program_id(0) == 0)
    def _():
        n_ref[:half, :] = (h0_ref[...] * gain_ref[...].astype(F32)).astype(BF16)
        n_ref[half:, :] = (h1_ref[...] * gain_ref[...].astype(F32)).astype(BF16)
        first = lax.broadcasted_iota(I32, ax_ref.shape, 1) < half
        straight = jnp.where(first, ax_ref[...], ay_ref[...])
        crossed = pltpu.roll(jnp.where(first, ay_ref[...], ax_ref[...]), half, 1)
        picked = jnp.where(slot_ref[0] == 1, straight, jnp.where(slot_ref[0] == 2, ad_ref[...], crossed))
        cols[...] = token_columns(picked, own_ref, ax_ref, ay_ref, ad_ref)

    for c in range(0, tile, chunk):
        z = jnp.dot(n_ref[...], w_ref[:, c:c + chunk], preferred_element_type=F32)
        g_ref[:, c:c + chunk] = softmax_grad(z, cols, pl.program_id(0) * tile + c)


def remote_grad(slot, h0, h1, gain, w, auxes, g_all, tile=768, chunk=256):
    half, h = h0.shape
    t, v = 2 * half, w.shape[1]
    return call(
        functools.partial(remote_body, tile=tile, chunk=chunk),
        grid_spec=pltpu.PrefetchScalarGridSpec(
            num_scalar_prefetch=1, grid=(pl.cdiv(v, tile),),
            in_specs=[whole((half, h)), whole((half, h)), whole((1, h)), pl.BlockSpec((h, tile), lambda j, slot_ref: (0, j))] + [whole((ROWS, t))] * 4 + [pl.BlockSpec(memory_space=pl.ANY)],
            out_specs=[pl.BlockSpec((t, tile), lambda j, slot_ref: (slot_ref[0], j)), whole((t, h))],
            scratch_shapes=[pltpu.VMEM((t, LANES), F32)],
        ),
        out_shape=[jax.ShapeDtypeStruct(g_all.shape, BF16), jax.ShapeDtypeStruct((t, h), BF16)],
        input_output_aliases={9: 0},
        cost=(2 * t * h * v, 2 * h * v + 2 * t * v),
    )(slot, h0, h1, gain, w, *auxes, g_all)


def wgrad_first_body(at_ref, *refs, tile, chunk, pieces):
    g_ref, out_ref, nts = refs[2 * pieces], refs[-3], refs[-2:]

    @pl.when(pl.program_id(0) == 0)
    def _():
        for k in range(2):
            first = 0
            for ref in refs[k * pieces:(k + 1) * pieces]:
                size = ref.shape[0]
                nts[k][:, first:first + size] = jnp.transpose(ref[...].astype(F32)).astype(BF16)
                first += size

    for c in range(0, tile, chunk):
        out_ref[:, c:c + chunk] = jnp.dot(nts[0][...], g_ref[:, c:c + chunk], preferred_element_type=F32)


def weight_grad_first(at, ns, g, tiles, tile=1792, chunk=256):
    k, _ = g.shape
    r = k // 4
    width = tiles * tile
    states = [pl.BlockSpec((n.shape[0], r), functools.partial(lambda which, j, at_ref: (0, at_ref[which]), which)) for which in range(2) for n in ns]
    return call(
        functools.partial(wgrad_first_body, tile=tile, chunk=chunk, pieces=len(ns)),
        grid_spec=pltpu.PrefetchScalarGridSpec(
            num_scalar_prefetch=1, grid=(tiles,), in_specs=states + [pl.BlockSpec((k, tile), lambda j, at_ref: (0, j))],
            out_specs=[pl.BlockSpec((r, tile), lambda j, at_ref: (0, j)), whole((r, k)), whole((r, k))],
        ),
        out_shape=[jax.ShapeDtypeStruct((r, width), F32)] + [jax.ShapeDtypeStruct((r, k), BF16)] * 2,
        cost=(2 * r * k * width, 2 * k * width + 4 * r * width),
    )(at, *ns, *ns, g)


def wgrad_body(nt_ref, g_ref, *rest, tile, chunk, with_add, with_sums):
    out_ref = rest[-3] if with_sums else rest[-1]
    if with_sums:
        gams, (sum0_ref, sum1_ref), (gam_ref, loss_ref) = rest[1:5], rest[5:7], rest[-2:]

        @pl.when(pl.program_id(0) == 0)
        def _():
            gam_ref[...] = (gams[0][...] + gams[1][...]) + (gams[2][...] + gams[3][...])
            loss_ref[...] = jnp.broadcast_to((sum0_ref[0:1, :] + sum1_ref[0:1, :]) / sum0_ref[1:2, :], loss_ref.shape)

    for c in range(0, tile, chunk):
        part = jnp.dot(nt_ref[...], g_ref[:, c:c + chunk], preferred_element_type=F32)
        out_ref[:, c:c + chunk] = part + rest[0][:, c:c + chunk] if with_add else part


def weight_grad(nt, g, first, tiles, add=None, into=None, sums=None, tile=1792, chunk=256):
    r, k = nt.shape
    v = g.shape[1]
    width = min(v - first * tile, tiles * tile)
    ins, aliases = [nt, g], {}
    specs = [whole((r, k)), pl.BlockSpec((k, tile), lambda j: (0, j + first))]
    out_specs, out_shape = pl.BlockSpec((r, tile), lambda j: (0, j)), jax.ShapeDtypeStruct((r, width), F32)
    if add is not None:
        ins.append(add)
        specs.append(pl.BlockSpec((r, tile), lambda j: (0, j)))
        out_specs, out_shape = pl.BlockSpec((r, tile), lambda j: (0, j + first)), jax.ShapeDtypeStruct((r, v), F32)
    if into is not None:
        aliases = {len(ins): 0}
        ins.append(into)
        specs.append(pl.BlockSpec(memory_space=pl.ANY))
    if sums is not None:
        ins.extend(sums)
        specs.extend(whole(a.shape) for a in sums)
        out_specs = [out_specs, whole(sums[0].shape), whole(sums[-1].shape)]
        out_shape = [out_shape, jax.ShapeDtypeStruct(sums[0].shape, F32), jax.ShapeDtypeStruct(sums[-1].shape, F32)]
    return call(
        functools.partial(wgrad_body, tile=tile, chunk=chunk, with_add=add is not None, with_sums=sums is not None),
        grid=(tiles,),
        in_specs=specs,
        out_specs=out_specs,
        out_shape=out_shape,
        input_output_aliases=aliases,
        cost=(2 * r * k * width, 2 * k * width + 4 * r * width),
    )(*ins)


def final_body(x_ref, inv_ref, gain_ref, mine_ref, other_ref, dh_ref, gam_ref):
    inv = inv_ref[...]
    hat = x_ref[...].astype(F32) * inv
    dn = mine_ref[...] + other_ref[...]
    prod = dn * hat

    @pl.when(pl.program_id(0) == 0)
    def _():
        gam_ref[...] = jnp.zeros(gam_ref.shape, F32)

    gam_ref[...] += jnp.sum(prod.reshape(-1, ROWS, prod.shape[1]), axis=0)
    d_hat = dn * gain_ref[...].astype(F32)
    dh_ref[...] = (inv * (d_hat - hat * jnp.mean(d_hat * hat, axis=-1, keepdims=True))).astype(BF16)


def final(x, inv, gain, mine, other, block=64):
    t, h = x.shape
    rows = pl.BlockSpec((block, h), lambda j: (j, 0))
    return call(
        final_body,
        grid=(t // block,),
        in_specs=[rows, pl.BlockSpec((block, 1), lambda j: (j, 0)), whole((1, h)), rows, rows],
        out_specs=[rows, whole((ROWS, h))],
        out_shape=[jax.ShapeDtypeStruct((t, h), BF16), jax.ShapeDtypeStruct((ROWS, h), F32)],
        cost=(10 * t * h, 12 * t * h),
    )(x, inv, gain, mine, other)


def solution(mesh):
    n_dp = mesh.shape["dp"]

    def swap(v, bits):
        return lax.ppermute(v, "dp", [(i, i ^ bits) for i in range(n_dp)])

    def swap_tp(v):
        return lax.ppermute(v, "tp", [(0, 1), (1, 0)])

    def step(hidden_in, labels, loss_mask, norm_gamma, w_local):
        tp, dp = lax.axis_index("tp").reshape(1), lax.axis_index("dp").reshape(1)
        gain = norm_gamma[None, :]
        low, high, n_own, inv, rows, cnt = prep(tp, hidden_in, gain, labels[None], loss_mask[None], w_local.shape[1])
        cnt_other = swap(cnt, 1)
        x_low, y_high = swap(low, 2), swap(high, 4)
        logits, stats = own_logits(n_own, w_local, rows)
        aux = combine(tp, stats, swap_tp(stats), rows, cnt, cnt_other)
        aux_x, aux_y, aux_d = swap(aux, 2), swap(aux, 4), swap(aux, 6)
        auxes = (aux, aux_x, aux_y, aux_d)
        x_low, y_high, low, high, auxes = lax.optimization_barrier((x_low, y_high, low, high, auxes))
        d_low, d_high = swap(x_low, 4), swap(y_high, 2)
        x_high, y_low = swap(high, 2), swap(low, 4)

        g_all, dn_mine, sums = own_grad(logits, w_local, auxes, 4)
        dn_other = swap_tp(dn_mine)
        sums_other = swap(sums, 1)
        ns = [n_own]
        for slot, h0, h1 in ((1, x_low, y_high), (2, d_low, d_high), (3, x_high, y_low)):
            g_all, n = remote_grad(jnp.array([slot], I32), h0, h1, gain, w_local, auxes, g_all)
            ns.append(n)

        at = jnp.concatenate([dp ^ 1, dp])
        p1, nt_other, nt_own = weight_grad_first(at, ns, g_all, 5)
        p1 = swap(p1, 1)
        p2 = swap(weight_grad(nt_other, g_all, 5, 4), 1)
        d_hidden, gam = final(hidden_in, inv, gain, dn_mine, dn_other)
        sums = (gam, swap(gam, 2), swap(gam, 4), swap(gam, 6), sums, sums_other)
        d_w_out, gam, loss = weight_grad(nt_own, g_all, 0, 5, add=p1, sums=sums)
        d_w_out = weight_grad(nt_own, g_all, 5, 4, add=p2, into=d_w_out)
        d_gamma = jnp.sum(gam + swap(gam, 1), axis=0)
        loss = loss[0, 0]
        return (loss, d_hidden, d_w_out, d_gamma)

    return jax.shard_map(step, mesh=mesh, in_specs=(P("dp", None), P("dp"), P("dp"), P(), P(None, "tp")), out_specs=(P(), P("dp", None), P("dp", "tp"), P()), check_vma=False)
```

time: 784 us -> 769 us (0.981)
  between operations: 8.81 us -> 0.71 us
    pallas_call x11 -> x10, Pallas kernels: 463 us -> 461 us  [the longest x3 249 us: remote_grad(): call(functools.partial(remote_body, tile=tile, chunk=chunk), grid_spec=pl...]
    ppermute x16 -> x17, starting transfers between devices: 17 us -> 16.3 us  [swap(): return lax.ppermute(v, 'dp', [(i, i ^ bits) for i in range(n_dp)])]
  transfers between devices with their start and end apart: 18 -> 19, of which waited for: 6 -> 7; matrix products, arithmetic and copies ran while one was open for 1% -> 0% of each run, Pallas kernels for 53% -> 56%
where the time goes in v2:
time: 769 us; the launch traced here: 768 us
  Pallas kernels  552 us (72%)
  waiting for transfers between devices  191 us (25%)
  starting transfers between devices  20 us (3%)
    pallas_call x3, Pallas kernels, remote_grad(): call(functools.partial(remote_body, tile=tile, chunk=chunk), grid_spec=pl...  249 us
    ppermute x2, waiting for transfers between devices, swap_tp(): return lax.ppermute(v, 'tp', [(0, 1), (1, 0)])  182 us
    pallas_call x1, Pallas kernels, own_grad(): call(functools.partial(back_body, tile=tile, vocab=v, rows=rows), grid=(p...  89 us
    pallas_call x1, Pallas kernels, own_logits(): call(functools.partial(own_body, tile=tile, block=block, vocab=v), grid=(...  82.8 us
    pallas_call x3, Pallas kernels, weight_grad(): call(functools.partial(wgrad_body, tile=tile, chunk=chunk, with_add=add i...  79.1 us
    pallas_call x1, Pallas kernels, weight_grad_first(): call(functools.partial(wgrad_first_body, tile=tile, chunk=chunk, pieces=l...  29 us
    ppermute x17, starting transfers between devices, swap(): return lax.ppermute(v, 'dp', [(i, i ^ bits) for i in range(n_dp)])  16.3 us
  transfers between devices with their start and end apart: 19, of which 7 were waited for; matrix products, arithmetic and copies ran while one was open for 0% of the time, Pallas kernels for 56%

profile of v2, /device:TPU:0, one launch (start us, length us, event | category | flops | bytes accessed | tf_op | source)
XLA Modules:
  0.0 768.1 jit_solution(1674536693184181757)
XLA Ops:
  0.6 1.3 broadcast_in_dim.9.gain_ref
  1.9 8.2 %shard_map.111 = (f32[256,4096]{1,0:T(8,128)}, f32[256,4096]{1,0:T(8,128)}, bf16[512,4096]{1,0:T(8,128)(2,1)}, f32[512,1]{1,0:T(8,128)}, f32[8,512]{1,0:T(8,128)}, /*index=5*/f32[8,128]{1,0:T(8,128)}) custom-call(s32[1]{0:T(128)} %bitcast.1.tp_ref, bf16[512,4096]{1,0:T(8,128)(2,1)} %x_ref.3, bf16[1,4096]{1,0:T(2,128)(2,1)} %broadcast_in_dim.9.gain_ref, ...), custom_call_target="tpu_custom_call" | custom-call | flops 16777216 | bytes 16777216 | tf_op jit(solution)/shard_map/pallas_call | solution.py:73
  10.2 3.2 collective-permute-start
  13.4 1.5 collective-permute-start.1
  14.9 82.8 %shard_map.112 = (f32[512,16000]{1,0:T(8,128)}, f32[8,512]{1,0:T(8,128)}) custom-call(bf16[512,4096]{1,0:T(8,128)(2,1)} %get-tuple-element.37.n_ref.refs_0_.refs_4_, bf16[4096,16000]{1,0:T(8,128)(2,1)} %w_ref.9, f32[8,512]{1,0:T(8,128)} %get-tuple-element.40.rows_ref), custom_call_target="tpu_custom_call" | custom-call | flops 67108864000 | bytes 163840000 | tf_op jit(solution)/shard_map/pallas_call | solution.py:132
  97.7 1.6 collective-permute-start.2
  99.3 1.5 collective-permute-done.3.cnt1_ref
  100.8 1.0 collective-permute-done.2.other_ref
  101.8 1.5 shard_map.113.own_ref
  103.3 0.5 collective-permute-start.4
  103.8 0.1 collective-permute-start.5
  103.9 2.9 collective-permute-start.6
  106.8 0.6 pad_add_fusion.at_ref
  107.4 0.0 collective-permute-done.4.ax_ref
  107.4 0.5 collective-permute-done.5.ay_ref
  107.9 1.0 collective-permute-done.6.ad_ref
  108.8 0.0 collective-permute-done.h0_ref
  108.8 0.0 collective-permute-done.1.h1_ref
  108.8 2.0 collective-permute-start.7
  110.8 1.5 collective-permute-start.8
  112.3 0.5 collective-permute-start.9
  112.8 0.1 collective-permute-start.10
  112.9 89.0 %shard_map.114 = (bf16[2048,16000]{1,0:T(8,128)(2,1)}, f32[512,4096]{1,0:T(8,128)}, f32[8,128]{1,0:T(8,128)}) custom-call(f32[512,16000]{1,0:T(8,128)} %get-tuple-element.49.z_ref, bf16[4096,16000]{1,0:T(8,128)(2,1)} %w_ref.9, f32[8,512]{1,0:T(8,128)} %shard_map.113.own_ref, f32[8,512]{1,0:T(8,128)} %collective-permute-done.4.ax_ref, ...), custom_call_target="tpu_custom_call" | custom-call | flops 67108864000 | bytes 180224000 | tf_op jit(solution)/shard_map/pallas_call | solution.py:191
  201.9 83.1 %shard_map.115 = (bf16[2048,16000]{1,0:T(8,128)(2,1)}, bf16[512,4096]{1,0:T(8,128)(2,1)}) custom-call(s32[1]{0:T(128)} %constant.19.clone.slot_ref, f32[256,4096]{1,0:T(8,128)} %collective-permute-done.h0_ref, f32[256,4096]{1,0:T(8,128)} %collective-permute-done.1.h1_ref, bf16[1,4096]{1,0:T(2,128)(2,1)} %broadcast_in_dim.9.gain_ref, ...), custom_call_target="tpu_custom_call", output_to_operand_aliasing={{0}: (9, {})} | custom-call | flops 67108864000 | bytes 147456000 | tf_op jit(solution)/shard_map/pallas_call | solution.py:223
  285.0 0.0 collective-permute-done.7.h0_ref
  285.0 0.0 collective-permute-done.8.h1_ref
  285.0 83.1 %shard_map.116 = (bf16[2048,16000]{1,0:T(8,128)(2,1)}, bf16[512,4096]{1,0:T(8,128)(2,1)}) custom-call(s32[1]{0:T(128)} %constant.20.clone.slot_ref, f32[256,4096]{1,0:T(8,128)} %collective-permute-done.7.h0_ref, f32[256,4096]{1,0:T(8,128)} %collective-permute-done.8.h1_ref, ...), custom_call_target="tpu_custom_call", output_to_operand_aliasing={{0}: (9, {})} | custom-call | flops 67108864000 | bytes 147456000 | tf_op jit(solution)/shard_map/pallas_call | solution.py:223
  368.0 0.0 collective-permute-done.10.h1_ref
  368.1 82.9 %shard_map.117 = (bf16[2048,16000]{1,0:T(8,128)(2,1)}, bf16[512,4096]{1,0:T(8,128)(2,1)}) custom-call(s32[1]{0:T(128)} %constant.21.clone.slot_ref, f32[256,4096]{1,0:T(8,128)} %collective-permute-done.9.h0_ref, f32[256,4096]{1,0:T(8,128)} %collective-permute-done.10.h1_ref, ...), custom_call_target="tpu_custom_call", output_to_operand_aliasing={{0}: (9, {})} | custom-call | flops 67108864000 | bytes 147456000 | tf_op jit(solution)/shard_map/pallas_call | solution.py:223
  451.0 29.0 %shard_map.118 = (f32[512,8960]{1,0:T(8,128)}, bf16[512,2048]{1,0:T(8,128)(2,1)}, bf16[512,2048]{1,0:T(8,128)(2,1)}) custom-call(s32[2]{0:T(128)} %pad_add_fusion.at_ref, bf16[512,4096]{1,0:T(8,128)(2,1)} %get-tuple-element.37.n_ref.refs_0_.refs_4_, bf16[512,4096]{1,0:T(8,128)(2,1)} %get-tuple-element.51.refs_1_.refs_5_, ...), custom_call_target="tpu_custom_call" | custom-call | flops 18790481920 | bytes 55050240 | tf_op jit(solution)/shard_map/pallas_call | solution.py:258
  480.0 0.0 collective-permute-start.11
  480.0 21.9 %shard_map.121 = f32[512,7040]{1,0:T(8,128)} custom-call(bf16[512,2048]{1,0:T(8,128)(2,1)} %get-tuple-element.67.nt_ref, bf16[2048,16000]{1,0:T(8,128)(2,1)} %get-tuple-element.58.refs_8_.g_ref), custom_call_target="tpu_custom_call" | custom-call | flops 14763950080 | bytes 43253760 | tf_op jit(solution)/shard_map/pallas_call | solution.py:304
  501.9 0.5 collective-permute-start.17
  502.4 2.1 collective-permute-start.12
  504.5 0.0 collective-permute-start.16
  504.5 181.0 %collective-permute-done.12.other_ref = f32[512,4096]{1,0:T(8,128)} collective-permute-done((f32[512,4096]{1,0:T(8,128)}, f32[512,4096]{1,0:T(8,128)}, u32[]{:S(2)}, u32[]{:S(2)}) %collective-permute-start.12) | collective-permute-done | bytes 8388640 | tf_op jit(solution)/shard_map/ppermute | solution.py:350
  685.4 12.8 %shard_map.119 = (bf16[512,4096]{1,0:T(8,128)(2,1)}, f32[8,4096]{1,0:T(8,128)}) custom-call(bf16[512,4096]{1,0:T(8,128)(2,1)} %x_ref.3, f32[512,1]{1,0:T(8,128)} %get-tuple-element.61.inv_ref, bf16[1,4096]{1,0:T(2,128)(2,1)} %broadcast_in_dim.9.gain_ref, f32[512,4096]{1,0:T(8,128)} %get-tuple-element.62.mine_ref, f32[512,4096]{1,0:T(8,128)} %collective-permute-done.12.other_ref), custom_call_target="tpu_custom_call" | custom-call | flops 20971520 | bytes 25165824 | tf_op jit(solution)/shard_map/pallas_call | solution.py:333
  698.3 1.5 collective-permute-start.13
  699.8 1.6 collective-permute-start.14
  701.4 0.4 collective-permute-start.15
  701.8 2.6 collective-permute-done.13.rest_2_
  704.3 3.6 collective-permute-done.14.rest_3_
  707.9 0.0 collective-permute-done.15.rest_4_
  707.9 31.9 %shard_map.120 = (f32[512,16000]{1,0:T(8,128)}, f32[8,4096]{1,0:T(8,128)}, f32[8,128]{1,0:T(8,128)}) custom-call(bf16[512,2048]{1,0:T(8,128)(2,1)} %get-tuple-element.59.nt_ref, bf16[2048,16000]{1,0:T(8,128)(2,1)} %get-tuple-element.58.refs_8_.g_ref, f32[512,8960]{1,0:T(8,128)} %collective-permute-done.11.rest_0_, f32[8,4096]{1,0:T(8,128)} %get-tuple-element.63.rest_1_, ...), custom_call_target="tpu_custom_call" | custom-call | flops 18790481920 | bytes 55050240 | tf_op jit(solution)/shard_map/pallas_call | solution.py:304
  739.8 0.0 collective-permute-start.18
  739.9 25.4 %shard_map.122 = f32[512,16000]{1,0:T(8,128)} custom-call(bf16[512,2048]{1,0:T(8,128)(2,1)} %get-tuple-element.59.nt_ref, bf16[2048,16000]{1,0:T(8,128)(2,1)} %get-tuple-element.58.refs_8_.g_ref, f32[512,7040]{1,0:T(8,128)} %collective-permute-done.17.rest_0_, f32[512,16000]{1,0:T(8,128)} %get-tuple-element.68.rest_1_), custom_call_target="tpu_custom_call", output_to_operand_aliasing={{}: (3, {})} | custom-call | flops 14763950080 | bytes 43253760 | tf_op jit(solution)/shard_map/pallas_call | solution.py:304
  765.2 1.2 slice.3
  766.4 1.6 add_reduce_fusion
  (6 shorter events, 0.0 us)
Async XLA Ops:
  10.2 98.6 %collective-permute-start = (f32[256,4096]{1,0:T(8,128)}, f32[256,4096]{1,0:T(8,128)}, u32[]{:S(2)}, u32[]{:S(2)}) collective-permute-start(f32[256,4096]{1,0:T(8,128)} %get-tuple-element.55), channel_id=1, source_target_pairs={{0,2},{1,3},{2,0},{3,1},{4,6},{5,7},{6,4},{7,5},{8,10},{9,11},{10,... | collective-permute-start | bytes 12582920 | tf_op jit(solution)/shard_map/ppermute | solution.py:347
  13.4 95.4 %collective-permute-start.1 = (f32[256,4096]{1,0:T(8,128)}, f32[256,4096]{1,0:T(8,128)}, u32[]{:S(2)}, u32[]{:S(2)}) collective-permute-start(f32[256,4096]{1,0:T(8,128)} %get-tuple-element.54), channel_id=1, source_target_pairs={{0,4},{1,5},{2,6},{3,7},{4,0},{5,1},{6,2},{7,3},{8,12},{9,13},{10,... | collective-permute-start | bytes 12582920 | tf_op jit(solution)/shard_map/ppermute | solution.py:347
  97.7 4.1 collective-permute-start.2
  99.3 1.5 collective-permute-start.3
  103.3 4.1 collective-permute-start.4
  103.8 4.1 collective-permute-start.5
  103.9 5.0 collective-permute-start.6
  108.8 176.1 %collective-permute-start.7 = (f32[256,4096]{1,0:T(8,128)}, f32[256,4096]{1,0:T(8,128)}, u32[]{:S(2)}, u32[]{:S(2)}) collective-permute-start(f32[256,4096]{1,0:T(8,128)} %collective-permute-done.h0_ref), channel_id=1, source_target_pairs={{0,4},{1,5},{2,6},{3,7},{4,0},{5,1},{6,2},{7,3},{8,12},{9,13},{10,... | collective-permute-start | bytes 12582920 | tf_op jit(solution)/shard_map/ppermute | solution.py:347
  110.8 174.2 %collective-permute-start.8 = (f32[256,4096]{1,0:T(8,128)}, f32[256,4096]{1,0:T(8,128)}, u32[]{:S(2)}, u32[]{:S(2)}) collective-permute-start(f32[256,4096]{1,0:T(8,128)} %collective-permute-done.1.h1_ref), channel_id=1, source_target_pairs={{0,2},{1,3},{2,0},{3,1},{4,6},{5,7},{6,4},{7,5},{8,10},{9,11},{10,... | collective-permute-start | bytes 12582920 | tf_op jit(solution)/shard_map/ppermute | solution.py:347
  112.3 255.8 %collective-permute-start.9 = (f32[256,4096]{1,0:T(8,128)}, f32[256,4096]{1,0:T(8,128)}, u32[]{:S(2)}, u32[]{:S(2)}) collective-permute-start(f32[256,4096]{1,0:T(8,128)} %get-tuple-element.54), channel_id=1, source_target_pairs={{0,2},{1,3},{2,0},{3,1},{4,6},{5,7},{6,4},{7,5},{8,10},{9,11},{10,... | collective-permute-start | bytes 12582920 | tf_op jit(solution)/shard_map/ppermute | solution.py:347
  112.8 255.2 %collective-permute-start.10 = (f32[256,4096]{1,0:T(8,128)}, f32[256,4096]{1,0:T(8,128)}, u32[]{:S(2)}, u32[]{:S(2)}) collective-permute-start(f32[256,4096]{1,0:T(8,128)} %get-tuple-element.55), channel_id=1, source_target_pairs={{0,4},{1,5},{2,6},{3,7},{4,0},{5,1},{6,2},{7,3},{8,12},{9,13},{10,... | collective-permute-start | bytes 12582920 | tf_op jit(solution)/shard_map/ppermute | solution.py:347
  480.0 227.9 %collective-permute-start.11 = (f32[512,8960]{1,0:T(8,128)}, f32[512,8960]{1,0:T(8,128)}, u32[]{:S(2)}, u32[]{:S(2)}) collective-permute-start(f32[512,8960]{1,0:T(8,128)} %get-tuple-element.60), channel_id=1, source_target_pairs={{0,1},{1,0},{2,3},{3,2},{4,5},{5,4},{6,7},{7,6},{8,9},{9,8},{10,11... | collective-permute-start | bytes 55050248 | tf_op jit(solution)/shard_map/ppermute | solution.py:347
  501.9 238.0 %collective-permute-start.17 = (f32[512,7040]{1,0:T(8,128)}, f32[512,7040]{1,0:T(8,128)}, u32[]{:S(2)}, u32[]{:S(2)}) collective-permute-start(f32[512,7040]{1,0:T(8,128)} %shard_map.121), channel_id=1, source_target_pairs={{0,1},{1,0},{2,3},{3,2},{4,5},{5,4},{6,7},{7,6},{8,9},{9,8},{10,11... | collective-permute-start | bytes 43253768 | tf_op jit(solution)/shard_map/ppermute | solution.py:347
  502.4 183.1 %collective-permute-start.12 = (f32[512,4096]{1,0:T(8,128)}, f32[512,4096]{1,0:T(8,128)}, u32[]{:S(2)}, u32[]{:S(2)}) collective-permute-start(f32[512,4096]{1,0:T(8,128)} %get-tuple-element.62.mine_ref), channel_id=1, source_target_pairs={{0,8},{8,0},{1,9},{9,1},{2,10},{10,2},{3,11},{11,3},{4,12},{12,4},... | collective-permute-start | bytes 25165832 | tf_op jit(solution)/shard_map/ppermute | solution.py:350
  504.5 196.9 %collective-permute-start.16 = (f32[8,128]{1,0:T(8,128)}, f32[8,128]{1,0:T(8,128)}, u32[]{:S(2)}, u32[]{:S(2)}) collective-permute-start(f32[8,128]{1,0:T(8,128)} %get-tuple-element.64.rest_5_), channel_id=1, source_target_pairs={{0,1},{1,0},{2,3},{3,2},{4,5},{5,4},{6,7},{7,6},{8,9},{9,8},{10,11... | collective-permute-start | bytes 12296 | tf_op jit(solution)/shard_map/ppermute | solution.py:347
  698.3 6.1 collective-permute-start.13
  699.8 8.1 %collective-permute-start.14 = (f32[8,4096]{1,0:T(8,128)}, f32[8,4096]{1,0:T(8,128)}, u32[]{:S(2)}, u32[]{:S(2)}) collective-permute-start(f32[8,4096]{1,0:T(8,128)} %get-tuple-element.63.rest_1_), channel_id=1, source_target_pairs={{0,4},{1,5},{2,6},{3,7},{4,0},{5,1},{6,2},{7,3},{8,12},{9,13},{10,... | collective-permute-start | bytes 393224 | tf_op jit(solution)/shard_map/ppermute | solution.py:347
  701.4 6.5 collective-permute-start.15
  739.8 26.6 %collective-permute-start.18 = (f32[8,4096]{1,0:T(8,128)}, f32[8,4096]{1,0:T(8,128)}, u32[]{:S(2)}, u32[]{:S(2)}) collective-permute-start(f32[8,4096]{1,0:T(8,128)} %get-tuple-element.69), channel_id=1, source_target_pairs={{0,1},{1,0},{2,3},{3,2},{4,5},{5,4},{6,7},{7,6},{8,9},{9,8},{10,11... | collective-permute-start | bytes 393224 | tf_op jit(solution)/shard_map/ppermute | solution.py:347

commit v3 on v2

--- a/solution.py
+++ b/solution.py
@@ -12,6 +12,7 @@
 VMEM_LIMIT = 64 * 1024 * 1024 - 64 * 1024
 LANES = 128
 ROWS = 8
+HEAD = 10240
 NT = (((1,), (1,)), ((), ()))
 
 
@@ -163,8 +164,9 @@
     )(tp, mine, other, rows, cnt0, cnt1)
 
 
-def back_body(z_ref, w_ref, own_ref, ax_ref, ay_ref, ad_ref, g_ref, dn_ref, sum_ref, cols, *, tile, vocab, rows):
+def back_body(z_ref, w_ref, own_ref, ax_ref, ay_ref, ad_ref, g_ref, dn_ref, sum_ref, low_ref, high_ref, cols, *, tile, vocab, rows):
     j = pl.program_id(0)
+    half = low_ref.shape[0]
 
     @pl.when(j == 0)
     def _():
@@ -180,20 +182,24 @@
         z_ref[:, width:] = jnp.zeros((z_ref.shape[0], tile - width), F32)
         w_ref[:, width:] = jnp.zeros((w_ref.shape[0], tile - width), BF16)
 
-    g_ref[...] = softmax_grad(z_ref[...], cols, j * tile)
+    g = softmax_grad(z_ref[...], cols, j * tile)
+    g_ref[...] = g
+    low_ref[...] = g[:half].astype(F32)
+    high_ref[...] = g[half:].astype(F32)
     for c in range(0, w_ref.shape[0], rows):
         dn_ref[:, c:c + rows] += lax.dot_general(g_ref[...], w_ref[c:c + rows, :], NT, preferred_element_type=F32)
 
 
 def own_grad(z, w, auxes, slots, tile=1024, rows=1024):
     t, v = z.shape
+    tail = pl.BlockSpec((t // 2, tile), lambda j: (0, jnp.maximum(j - HEAD // tile, 0)))
     h = w.shape[0]
     return call(
         functools.partial(back_body, tile=tile, vocab=v, rows=rows),
         grid=(pl.cdiv(v, tile),),
         in_specs=[pl.BlockSpec((t, tile), lambda j: (0, j)), pl.BlockSpec((h, tile), lambda j: (0, j))] + [whole((ROWS, t))] * 4,
-        out_specs=[pl.BlockSpec((t, tile), lambda j: (0, j)), whole((t, h)), whole((ROWS, LANES))],
-        out_shape=[jax.ShapeDtypeStruct((slots * t, v), BF16), jax.ShapeDtypeStruct((t, h), F32), jax.ShapeDtypeStruct((ROWS, LANES), F32)],
+        out_specs=[pl.BlockSpec((t, tile), lambda j: (0, j)), whole((t, h)), whole((ROWS, LANES)), tail, tail],
+        out_shape=[jax.ShapeDtypeStruct((slots * t, v), BF16), jax.ShapeDtypeStruct((t, h), F32), jax.ShapeDtypeStruct((ROWS, LANES), F32)] + [jax.ShapeDtypeStruct((t // 2, v - HEAD), F32)] * 2,
         scratch_shapes=[pltpu.VMEM((t, LANES), F32)],
         cost=(2 * t * h * v, 2 * h * v + 6 * t * v),
     )(z, w, *auxes)
@@ -212,26 +218,48 @@
         picked = jnp.where(slot_ref[0] == 1, straight, jnp.where(slot_ref[0] == 2, ad_ref[...], crossed))
         cols[...] = token_columns(picked, own_ref, ax_ref, ay_ref, ad_ref)
 
-    for c in range(0, tile, chunk):
-        z = jnp.dot(n_ref[...], w_ref[:, c:c + chunk], preferred_element_type=F32)
-        g_ref[:, c:c + chunk] = softmax_grad(z, cols, pl.program_id(0) * tile + c)
-
-
-def remote_grad(slot, h0, h1, gain, w, auxes, g_all, tile=768, chunk=256):
+    @pl.when(pl.program_id(0) < slot_ref[1])
+    def _():
+        for c in range(0, tile, chunk):
+            z = jnp.dot(n_ref[...], w_ref[:, c:c + chunk], preferred_element_type=F32)
+            g_ref[:, c:c + chunk] = softmax_grad(z, cols, pl.program_id(0) * tile + c)
+
+
+def remote_grad(slot, width, h0, h1, gain, w, auxes, g_all, tile=768, chunk=256):
     half, h = h0.shape
     t, v = 2 * half, w.shape[1]
     return call(
         functools.partial(remote_body, tile=tile, chunk=chunk),
         grid_spec=pltpu.PrefetchScalarGridSpec(
             num_scalar_prefetch=1, grid=(pl.cdiv(v, tile),),
-            in_specs=[whole((half, h)), whole((half, h)), whole((1, h)), pl.BlockSpec((h, tile), lambda j, slot_ref: (0, j))] + [whole((ROWS, t))] * 4 + [pl.BlockSpec(memory_space=pl.ANY)],
-            out_specs=[pl.BlockSpec((t, tile), lambda j, slot_ref: (slot_ref[0], j)), whole((t, h))],
+            in_specs=[whole((half, h)), whole((half, h)), whole((1, h)), pl.BlockSpec((h, tile), lambda j, slot_ref: (0, jnp.minimum(j, slot_ref[1] - 1)))] + [whole((ROWS, t))] * 4 + [pl.BlockSpec(memory_space=pl.ANY)],
+            out_specs=[pl.BlockSpec((t, tile), lambda j, slot_ref: (slot_ref[0], jnp.minimum(j, slot_ref[1] - 1))), whole((t, h))],
             scratch_shapes=[pltpu.VMEM((t, LANES), F32)],
         ),
         out_shape=[jax.ShapeDtypeStruct(g_all.shape, BF16), jax.ShapeDtypeStruct((t, h), BF16)],
         input_output_aliases={9: 0},
         cost=(2 * t * h * v, 2 * h * v + 2 * t * v),
-    )(slot, h0, h1, gain, w, *auxes, g_all)
+    )(jnp.array([slot, pl.cdiv(width, tile)], I32), h0, h1, gain, w, *auxes, g_all)
+
+
+def place_body(h0_ref, h1_ref, _, g_ref):
+    half = h0_ref.shape[0]
+    g_ref[:half, :] = h0_ref[...].astype(BF16)
+    g_ref[half:, :] = h1_ref[...].astype(BF16)
+
+
+def place(h0, h1, g_all, slot, tile=1024):
+    half, width = h0.shape
+    part = pl.BlockSpec((half, tile), lambda j: (0, j))
+    return call(
+        place_body,
+        grid=(pl.cdiv(width, tile),),
+        in_specs=[part, part, pl.BlockSpec(memory_space=pl.ANY)],
+        out_specs=pl.BlockSpec((2 * half, tile), lambda j: (slot, j + HEAD // tile)),
+        out_shape=jax.ShapeDtypeStruct(g_all.shape, BF16),
+        input_output_aliases={2: 0},
+        cost=(4 * half * width, 12 * half * width),
+    )(h0, h1, g_all)
 
 
 def wgrad_first_body(at_ref, *refs, tile, chunk, pieces):
@@ -363,13 +391,16 @@
         d_low, d_high = swap(x_low, 4), swap(y_high, 2)
         x_high, y_low = swap(high, 2), swap(low, 4)
 
-        g_all, dn_mine, sums = own_grad(logits, w_local, auxes, 4)
+        g_all, dn_mine, sums, tail_low, tail_high = own_grad(logits, w_local, auxes, 4)
         dn_other = swap_tp(dn_mine)
         sums_other = swap(sums, 1)
+        tail_x, tail_y = swap(tail_high, 2), swap(tail_low, 4)
         ns = [n_own]
-        for slot, h0, h1 in ((1, x_low, y_high), (2, d_low, d_high), (3, x_high, y_low)):
-            g_all, n = remote_grad(jnp.array([slot], I32), h0, h1, gain, w_local, auxes, g_all)
+        vocab = w_local.shape[1]
+        for slot, width, h0, h1 in ((1, vocab, x_low, y_high), (2, vocab, d_low, d_high), (3, HEAD, x_high, y_low)):
+            g_all, n = remote_grad(slot, width, h0, h1, gain, w_local, auxes, g_all)
             ns.append(n)
+        g_all = place(tail_x, tail_y, g_all, 3)
 
         at = jnp.concatenate([dp ^ 1, dp])
         p1, nt_other, nt_own = weight_grad_first(at, ns, g_all, 5)

time: 769 us -> 760 us (0.988)
  Pallas kernels: 552 us -> 541 us
    pallas_call x3, Pallas kernels: 249 us -> 228 us  [remote_grad(): call(functools.partial(remote_body, tile=tile, chunk=chunk), grid_spec=pl...]
    pallas_call x0 -> x1, Pallas kernels: none -> 7.96 us  [place(): call(place_body, grid=(pl.cdiv(width, tile),), in_specs=[part, part, pl.B...]
    ppermute x17 -> x19, starting transfers between devices: 16.3 us -> 19.8 us  [swap(): return lax.ppermute(v, 'dp', [(i, i ^ bits) for i in range(n_dp)])]
  transfers between devices with their start and end apart: 19 -> 21, of which waited for: 7 -> 7; matrix products, arithmetic and copies ran while one was open for 0% -> 0% of each run, Pallas kernels for 56% -> 65%
where the time goes in v3:
time: 760 us; the launch traced here: 759 us
  Pallas kernels  541 us (71%)
  waiting for transfers between devices  190 us (25%)
  starting transfers between devices  23 us (3%)
    pallas_call x3, Pallas kernels, remote_grad(): call(functools.partial(remote_body, tile=tile, chunk=chunk), grid_spec=pl...  228 us
    ppermute x2, waiting for transfers between devices, swap_tp(): return lax.ppermute(v, 'tp', [(0, 1), (1, 0)])  182 us
    pallas_call x1, Pallas kernels, own_grad(): call(functools.partial(back_body, tile=tile, vocab=v, rows=rows), grid=(p...  91.1 us
    pallas_call x1, Pallas kernels, own_logits(): call(functools.partial(own_body, tile=tile, block=block, vocab=v), grid=(...  82.8 us
    pallas_call x3, Pallas kernels, weight_grad(): call(functools.partial(wgrad_body, tile=tile, chunk=chunk, with_add=add i...  79.5 us
    pallas_call x1, Pallas kernels, weight_grad_first(): call(functools.partial(wgrad_first_body, tile=tile, chunk=chunk, pieces=l...  29.3 us
    ppermute x19, starting transfers between devices, swap(): return lax.ppermute(v, 'dp', [(i, i ^ bits) for i in range(n_dp)])  19.8 us
  transfers between devices with their start and end apart: 21, of which 7 were waited for; matrix products, arithmetic and copies ran while one was open for 0% of the time, Pallas kernels for 65%

profile of v3, /device:TPU:0, one launch (start us, length us, event | category | flops | bytes accessed | tf_op | source)
XLA Modules:
  0.0 758.9 jit_solution(17977414855896146896)
XLA Ops:
  0.6 1.3 broadcast_in_dim.9.gain_ref
  1.9 8.3 %shard_map.111 = (f32[256,4096]{1,0:T(8,128)}, f32[256,4096]{1,0:T(8,128)}, bf16[512,4096]{1,0:T(8,128)(2,1)}, f32[512,1]{1,0:T(8,128)}, f32[8,512]{1,0:T(8,128)}, /*index=5*/f32[8,128]{1,0:T(8,128)}) custom-call(s32[1]{0:T(128)} %bitcast.1.tp_ref, bf16[512,4096]{1,0:T(8,128)(2,1)} %x_ref.3, bf16[1,4096]{1,0:T(2,128)(2,1)} %broadcast_in_dim.9.gain_ref, ...), custom_call_target="tpu_custom_call" | custom-call | flops 16777216 | bytes 16777216 | tf_op jit(solution)/shard_map/pallas_call | solution.py:74
  10.2 3.2 collective-permute-start
  13.4 1.5 collective-permute-start.1
  14.9 82.8 %shard_map.112 = (f32[512,16000]{1,0:T(8,128)}, f32[8,512]{1,0:T(8,128)}) custom-call(bf16[512,4096]{1,0:T(8,128)(2,1)} %get-tuple-element.39.n_ref.refs_0_.refs_4_, bf16[4096,16000]{1,0:T(8,128)(2,1)} %w_ref.9, f32[8,512]{1,0:T(8,128)} %get-tuple-element.42.rows_ref), custom_call_target="tpu_custom_call" | custom-call | flops 67108864000 | bytes 163840000 | tf_op jit(solution)/shard_map/pallas_call | solution.py:133
  97.8 1.6 collective-permute-start.2
  99.3 0.0 collective-permute-start.3
  99.3 1.5 collective-permute-done.3.cnt1_ref
  100.8 1.0 collective-permute-done.2.other_ref
  101.8 1.5 shard_map.113.own_ref
  103.3 0.5 collective-permute-start.4
  103.8 0.1 collective-permute-start.5
  103.9 2.9 collective-permute-start.6
  106.8 0.6 pad_add_fusion.at_ref
  107.4 0.0 collective-permute-done.4.ax_ref
  107.4 0.5 collective-permute-done.5.ay_ref
  107.9 1.0 collective-permute-done.6.ad_ref
  108.9 0.0 collective-permute-done.1.h1_ref
  108.9 2.0 collective-permute-start.7
  110.8 1.5 collective-permute-start.8
  112.3 0.5 collective-permute-start.9
  112.8 0.1 collective-permute-start.10
  112.9 91.1 %shard_map.114 = (bf16[2048,16000]{1,0:T(8,128)(2,1)}, f32[512,4096]{1,0:T(8,128)}, f32[8,128]{1,0:T(8,128)}, f32[256,5760]{1,0:T(8,128)}, f32[256,5760]{1,0:T(8,128)}) custom-call(f32[512,16000]{1,0:T(8,128)} %get-tuple-element.51.z_ref, bf16[4096,16000]{1,0:T(8,128)(2,1)} %w_ref.9, f32[8,512]{1,0:T(8,128)} %shard_map.113.own_ref, ...), custom_call_target="tpu_custom_call" | custom-call | flops 67108864000 | bytes 180224000 | tf_op jit(solution)/shard_map/pallas_call | solution.py:197
  204.0 1.9 collective-permute-start.11
  205.9 84.3 %shard_map.115 = (bf16[2048,16000]{1,0:T(8,128)(2,1)}, bf16[512,4096]{1,0:T(8,128)(2,1)}) custom-call(s32[2]{0:T(128)} %constant.19.clone.slot_ref, f32[256,4096]{1,0:T(8,128)} %collective-permute-done.h0_ref, f32[256,4096]{1,0:T(8,128)} %collective-permute-done.1.h1_ref, bf16[1,4096]{1,0:T(2,128)(2,1)} %broadcast_in_dim.9.gain_ref, ...), custom_call_target="tpu_custom_call", output_to_operand_aliasing={{0}: (9, {})} | custom-call | flops 67108864000 | bytes 147456000 | tf_op jit(solution)/shard_map/pallas_call | solution.py:231
  290.2 0.0 collective-permute-done.7.h0_ref
  290.2 1.6 collective-permute-start.12
  291.8 0.0 collective-permute-done.8.h1_ref
  291.8 83.9 %shard_map.116 = (bf16[2048,16000]{1,0:T(8,128)(2,1)}, bf16[512,4096]{1,0:T(8,128)(2,1)}) custom-call(s32[2]{0:T(128)} %constant.20.clone.slot_ref, f32[256,4096]{1,0:T(8,128)} %collective-permute-done.7.h0_ref, f32[256,4096]{1,0:T(8,128)} %collective-permute-done.8.h1_ref, ...), custom_call_target="tpu_custom_call", output_to_operand_aliasing={{0}: (9, {})} | custom-call | flops 67108864000 | bytes 147456000 | tf_op jit(solution)/shard_map/pallas_call | solution.py:231
  375.6 0.0 collective-permute-done.10.h1_ref
  375.7 59.6 %shard_map.117 = (bf16[2048,16000]{1,0:T(8,128)(2,1)}, bf16[512,4096]{1,0:T(8,128)(2,1)}) custom-call(s32[2]{0:T(128)} %constant.21.clone.slot_ref, f32[256,4096]{1,0:T(8,128)} %collective-permute-done.9.h0_ref, f32[256,4096]{1,0:T(8,128)} %collective-permute-done.10.h1_ref, ...), custom_call_target="tpu_custom_call", output_to_operand_aliasing={{0}: (9, {})} | custom-call | flops 67108864000 | bytes 147456000 | tf_op jit(solution)/shard_map/pallas_call | solution.py:231
  435.3 8.0 %shard_map.118.refs_8_.g_ref = bf16[2048,16000]{1,0:T(8,128)(2,1)} custom-call(f32[256,5760]{1,0:T(8,128)} %collective-permute-done.11.h0_ref, f32[256,5760]{1,0:T(8,128)} %collective-permute-done.12.h1_ref, bf16[2048,16000]{1,0:T(8,128)(2,1)} %get-tuple-element.62._), custom_call_target="tpu_custom_call", output_to_operand_aliasing={{}: (2, {})} | custom-call | flops 5898240 | bytes 17694720 | tf_op jit(solution)/shard_map/pallas_call | solution.py:254
  443.2 29.3 %shard_map.119 = (f32[512,8960]{1,0:T(8,128)}, bf16[512,2048]{1,0:T(8,128)(2,1)}, bf16[512,2048]{1,0:T(8,128)(2,1)}) custom-call(s32[2]{0:T(128)} %pad_add_fusion.at_ref, bf16[512,4096]{1,0:T(8,128)(2,1)} %get-tuple-element.39.n_ref.refs_0_.refs_4_, bf16[512,4096]{1,0:T(8,128)(2,1)} %get-tuple-element.53.refs_1_.refs_5_, ...), custom_call_target="tpu_custom_call" | custom-call | flops 18790481920 | bytes 55050240 | tf_op jit(solution)/shard_map/pallas_call | solution.py:286
  472.5 21.8 %shard_map.122 = f32[512,7040]{1,0:T(8,128)} custom-call(bf16[512,2048]{1,0:T(8,128)(2,1)} %get-tuple-element.71.nt_ref, bf16[2048,16000]{1,0:T(8,128)(2,1)} %shard_map.118.refs_8_.g_ref), custom_call_target="tpu_custom_call" | custom-call | flops 14763950080 | bytes 43253760 | tf_op jit(solution)/shard_map/pallas_call | solution.py:332
  494.4 0.5 collective-permute-start.19
  494.8 1.7 collective-permute-start.14
  496.5 181.0 %collective-permute-done.14.other_ref = f32[512,4096]{1,0:T(8,128)} collective-permute-done((f32[512,4096]{1,0:T(8,128)}, f32[512,4096]{1,0:T(8,128)}, u32[]{:S(2)}, u32[]{:S(2)}) %collective-permute-start.14) | collective-permute-done | bytes 8388640 | tf_op jit(solution)/shard_map/ppermute | solution.py:378
  677.5 12.8 %shard_map.120 = (bf16[512,4096]{1,0:T(8,128)(2,1)}, f32[8,4096]{1,0:T(8,128)}) custom-call(bf16[512,4096]{1,0:T(8,128)(2,1)} %x_ref.3, f32[512,1]{1,0:T(8,128)} %get-tuple-element.65.inv_ref, bf16[1,4096]{1,0:T(2,128)(2,1)} %broadcast_in_dim.9.gain_ref, f32[512,4096]{1,0:T(8,128)} %get-tuple-element.66.mine_ref, f32[512,4096]{1,0:T(8,128)} %collective-permute-done.14.other_ref), custom_call_target="tpu_custom_call" | custom-call | flops 20971520 | bytes 25165824 | tf_op jit(solution)/shard_map/pallas_call | solution.py:361
  690.4 0.4 collective-permute-start.15
  690.8 0.5 collective-permute-start.16
  691.3 2.6 collective-permute-start.17
  693.9 2.8 collective-permute-done.15.rest_2_
  696.7 1.7 collective-permute-done.16.rest_3_
  698.4 32.1 %shard_map.121 = (f32[512,16000]{1,0:T(8,128)}, f32[8,4096]{1,0:T(8,128)}, f32[8,128]{1,0:T(8,128)}) custom-call(bf16[512,2048]{1,0:T(8,128)(2,1)} %get-tuple-element.63.nt_ref, bf16[2048,16000]{1,0:T(8,128)(2,1)} %shard_map.118.refs_8_.g_ref, f32[512,8960]{1,0:T(8,128)} %collective-permute-done.13.rest_0_, f32[8,4096]{1,0:T(8,128)} %get-tuple-element.67.rest_1_, ...), custom_call_target="tpu_custom_call" | custom-call | flops 18790481920 | bytes 55050240 | tf_op jit(solution)/shard_map/pallas_call | solution.py:332
  730.5 0.0 collective-permute-start.20
  730.6 25.5 %shard_map.123 = f32[512,16000]{1,0:T(8,128)} custom-call(bf16[512,2048]{1,0:T(8,128)(2,1)} %get-tuple-element.63.nt_ref, bf16[2048,16000]{1,0:T(8,128)(2,1)} %shard_map.118.refs_8_.g_ref, f32[512,7040]{1,0:T(8,128)} %collective-permute-done.19.rest_0_, f32[512,16000]{1,0:T(8,128)} %get-tuple-element.72.rest_1_), custom_call_target="tpu_custom_call", output_to_operand_aliasing={{}: (3, {})} | custom-call | flops 14763950080 | bytes 43253760 | tf_op jit(solution)/shard_map/pallas_call | solution.py:332
  756.1 1.2 slice.3
  757.3 1.6 add_reduce_fusion
  (11 shorter events, 0.0 us)
Async XLA Ops:
  10.2 98.6 %collective-permute-start = (f32[256,4096]{1,0:T(8,128)}, f32[256,4096]{1,0:T(8,128)}, u32[]{:S(2)}, u32[]{:S(2)}) collective-permute-start(f32[256,4096]{1,0:T(8,128)} %get-tuple-element.57), channel_id=1, source_target_pairs={{0,2},{1,3},{2,0},{3,1},{4,6},{5,7},{6,4},{7,5},{8,10},{9,11},{10,... | collective-permute-start | bytes 12582920 | tf_op jit(solution)/shard_map/ppermute | solution.py:375
  13.4 95.4 %collective-permute-start.1 = (f32[256,4096]{1,0:T(8,128)}, f32[256,4096]{1,0:T(8,128)}, u32[]{:S(2)}, u32[]{:S(2)}) collective-permute-start(f32[256,4096]{1,0:T(8,128)} %get-tuple-element.56), channel_id=1, source_target_pairs={{0,4},{1,5},{2,6},{3,7},{4,0},{5,1},{6,2},{7,3},{8,12},{9,13},{10,... | collective-permute-start | bytes 12582920 | tf_op jit(solution)/shard_map/ppermute | solution.py:375
  97.8 4.1 collective-permute-start.2
  99.3 1.5 collective-permute-start.3
  103.3 4.1 collective-permute-start.4
  103.8 4.1 collective-permute-start.5
  103.9 5.0 collective-permute-start.6
  108.9 181.3 %collective-permute-start.7 = (f32[256,4096]{1,0:T(8,128)}, f32[256,4096]{1,0:T(8,128)}, u32[]{:S(2)}, u32[]{:S(2)}) collective-permute-start(f32[256,4096]{1,0:T(8,128)} %collective-permute-done.h0_ref), channel_id=1, source_target_pairs={{0,4},{1,5},{2,6},{3,7},{4,0},{5,1},{6,2},{7,3},{8,12},{9,13},{10,... | collective-permute-start | bytes 12582920 | tf_op jit(solution)/shard_map/ppermute | solution.py:375
  110.8 180.9 %collective-permute-start.8 = (f32[256,4096]{1,0:T(8,128)}, f32[256,4096]{1,0:T(8,128)}, u32[]{:S(2)}, u32[]{:S(2)}) collective-permute-start(f32[256,4096]{1,0:T(8,128)} %collective-permute-done.1.h1_ref), channel_id=1, source_target_pairs={{0,2},{1,3},{2,0},{3,1},{4,6},{5,7},{6,4},{7,5},{8,10},{9,11},{10,... | collective-permute-start | bytes 12582920 | tf_op jit(solution)/shard_map/ppermute | solution.py:375
  112.3 263.3 %collective-permute-start.9 = (f32[256,4096]{1,0:T(8,128)}, f32[256,4096]{1,0:T(8,128)}, u32[]{:S(2)}, u32[]{:S(2)}) collective-permute-start(f32[256,4096]{1,0:T(8,128)} %get-tuple-element.56), channel_id=1, source_target_pairs={{0,2},{1,3},{2,0},{3,1},{4,6},{5,7},{6,4},{7,5},{8,10},{9,11},{10,... | collective-permute-start | bytes 12582920 | tf_op jit(solution)/shard_map/ppermute | solution.py:375
  112.8 262.8 %collective-permute-start.10 = (f32[256,4096]{1,0:T(8,128)}, f32[256,4096]{1,0:T(8,128)}, u32[]{:S(2)}, u32[]{:S(2)}) collective-permute-start(f32[256,4096]{1,0:T(8,128)} %get-tuple-element.57), channel_id=1, source_target_pairs={{0,4},{1,5},{2,6},{3,7},{4,0},{5,1},{6,2},{7,3},{8,12},{9,13},{10,... | collective-permute-start | bytes 12582920 | tf_op jit(solution)/shard_map/ppermute | solution.py:375
  204.0 231.3 %collective-permute-start.11 = (f32[256,5760]{1,0:T(8,128)}, f32[256,5760]{1,0:T(8,128)}, u32[]{:S(2)}, u32[]{:S(2)}) collective-permute-start(f32[256,5760]{1,0:T(8,128)} %get-tuple-element.60), channel_id=1, source_target_pairs={{0,2},{1,3},{2,0},{3,1},{4,6},{5,7},{6,4},{7,5},{8,10},{9,11},{10,... | collective-permute-start | bytes 17694728 | tf_op jit(solution)/shard_map/ppermute | solution.py:375
  290.2 145.1 %collective-permute-start.12 = (f32[256,5760]{1,0:T(8,128)}, f32[256,5760]{1,0:T(8,128)}, u32[]{:S(2)}, u32[]{:S(2)}) collective-permute-start(f32[256,5760]{1,0:T(8,128)} %get-tuple-element.61), channel_id=1, source_target_pairs={{0,4},{1,5},{2,6},{3,7},{4,0},{5,1},{6,2},{7,3},{8,12},{9,13},{10,... | collective-permute-start | bytes 17694728 | tf_op jit(solution)/shard_map/ppermute | solution.py:375
  472.5 225.9 %collective-permute-start.13 = (f32[512,8960]{1,0:T(8,128)}, f32[512,8960]{1,0:T(8,128)}, u32[]{:S(2)}, u32[]{:S(2)}) collective-permute-start(f32[512,8960]{1,0:T(8,128)} %get-tuple-element.64), channel_id=1, source_target_pairs={{0,1},{1,0},{2,3},{3,2},{4,5},{5,4},{6,7},{7,6},{8,9},{9,8},{10,11... | collective-permute-start | bytes 55050248 | tf_op jit(solution)/shard_map/ppermute | solution.py:375
  494.4 236.2 %collective-permute-start.19 = (f32[512,7040]{1,0:T(8,128)}, f32[512,7040]{1,0:T(8,128)}, u32[]{:S(2)}, u32[]{:S(2)}) collective-permute-start(f32[512,7040]{1,0:T(8,128)} %shard_map.122), channel_id=1, source_target_pairs={{0,1},{1,0},{2,3},{3,2},{4,5},{5,4},{6,7},{7,6},{8,9},{9,8},{10,11... | collective-permute-start | bytes 43253768 | tf_op jit(solution)/shard_map/ppermute | solution.py:375
  494.8 182.7 %collective-permute-start.14 = (f32[512,4096]{1,0:T(8,128)}, f32[512,4096]{1,0:T(8,128)}, u32[]{:S(2)}, u32[]{:S(2)}) collective-permute-start(f32[512,4096]{1,0:T(8,128)} %get-tuple-element.66.mine_ref), channel_id=1, source_target_pairs={{0,8},{8,0},{1,9},{9,1},{2,10},{10,2},{3,11},{11,3},{4,12},{12,4},... | collective-permute-start | bytes 25165832 | tf_op jit(solution)/shard_map/ppermute | solution.py:378
  496.5 194.8 %collective-permute-start.18 = (f32[8,128]{1,0:T(8,128)}, f32[8,128]{1,0:T(8,128)}, u32[]{:S(2)}, u32[]{:S(2)}) collective-permute-start(f32[8,128]{1,0:T(8,128)} %get-tuple-element.68.rest_5_), channel_id=1, source_target_pairs={{0,1},{1,0},{2,3},{3,2},{4,5},{5,4},{6,7},{7,6},{8,9},{9,8},{10,11... | collective-permute-start | bytes 12296 | tf_op jit(solution)/shard_map/ppermute | solution.py:375
  690.4 6.3 collective-permute-start.15
  690.8 7.6 %collective-permute-start.16 = (f32[8,4096]{1,0:T(8,128)}, f32[8,4096]{1,0:T(8,128)}, u32[]{:S(2)}, u32[]{:S(2)}) collective-permute-start(f32[8,4096]{1,0:T(8,128)} %get-tuple-element.67.rest_1_), channel_id=1, source_target_pairs={{0,4},{1,5},{2,6},{3,7},{4,0},{5,1},{6,2},{7,3},{8,12},{9,13},{10,... | collective-permute-start | bytes 393224 | tf_op jit(solution)/shard_map/ppermute | solution.py:375
  691.3 7.1 collective-permute-start.17
  730.5 26.8 %collective-permute-start.20 = (f32[8,4096]{1,0:T(8,128)}, f32[8,4096]{1,0:T(8,128)}, u32[]{:S(2)}, u32[]{:S(2)}) collective-permute-start(f32[8,4096]{1,0:T(8,128)} %get-tuple-element.73), channel_id=1, source_target_pairs={{0,1},{1,0},{2,3},{3,2},{4,5},{5,4},{6,7},{7,6},{8,9},{9,8},{10,11... | collective-permute-start | bytes 393224 | tf_op jit(solution)/shard_map/ppermute | solution.py:375
